TPU v7x, 128 devices: a whole 4x4x4 slice. The times are simulated.
128 devices in a mesh: ma: 16 (over x, y), lev: 8 (over z, core).
Axes of the slice: x: 4, y: 4, z: 4, core: 2. Of those that a mesh axis runs over, the one named last changes fastest.
Arguments:
- spectral_state: float32 [1280, 2, 32, 1280], P('ma', None, None, 'lev'), may hold values from -6 to 6
- forcing_noise: bfloat16 [1280, 2, 32, 1280], P('ma', None, None, 'lev'), may hold values from -6 to 6
- decay_rate: float32 [32], replicated, may hold values from 0.3 to 0.95
- amplitude: float32 [1280], P('lev'), may hold values from 0.2 to 2
- legendre: bfloat16 [1280, 1280, 640], P('ma', 'lev'), may hold values from -0.0048828125 to 0.0048828125
- wave_of_slot: int32 [1280], replicated, may hold values from 0 to 1279, each once
- lat_of_row: int32 [1280], replicated, may hold values from 0 to 1279, each once
Outputs:
- new_state: float32 [1280, 2, 32, 1280], P('ma', None, None, 'lev')
- pattern: bfloat16 [32, 1280, 2560], P('lev', 'ma')
Inputs may be any that keep to these rules, and one draw needn't show every extreme that they name: `wave_of_slot`: each zonal wavenumber is held by exactly one slot. `lat_of_row`: each latitude is held by exactly one row.
All inputs are finite; a program needn't handle non-finite values.
Results may differ from a plain program's by a relative error of at most 0.014.
Values may be sent and summed in bfloat16 or wider, within the bound.
A program may use at most 192 MiB of HBM per device.

v0:
```python
import math

import jax
import jax.numpy as jnp
from jax import lax
from jax.sharding import PartitionSpec as P

NLON = 2560


def build_table(wavenum, width):
    column = jnp.arange(width, dtype=jnp.int32)
    product = wavenum[:, None] * column[None, :] % width
    phase_angle = product.astype(jnp.float32) * jnp.float32(2.0 * math.pi / width)
    factor = jnp.where(wavenum == 0, jnp.float32(1.0), jnp.float32(2.0))[:, None]
    stacked = jnp.stack([factor * jnp.cos(phase_angle), -factor * jnp.sin(phase_angle)], axis=1)
    return stacked.astype(jnp.bfloat16)


def body(spectral_state, forcing_noise, decay_rate, amplitude, legendre, wave_of_slot, lat_of_row):
    slot_count = spectral_state.shape[0]
    level_count = spectral_state.shape[2]
    width_n = spectral_state.shape[3]
    lat_count = lat_of_row.shape[0]
    first_slot = lax.axis_index("ma") * slot_count
    wavenum = lax.dynamic_slice_in_dim(wave_of_slot, first_slot, slot_count)
    total_n = lax.axis_index("lev") * width_n + jnp.arange(width_n, dtype=jnp.int32)
    valid_mask = total_n[None, :] >= wavenum[:, None]
    updated = decay_rate[None, None, :, None] * spectral_state + amplitude[
        None, None, None, :
    ] * forcing_noise.astype(jnp.float32)
    new_state = jnp.where(valid_mask[:, None, None, :], updated, jnp.float32(0.0))
    spectral = new_state.astype(jnp.bfloat16).reshape(slot_count, 2 * level_count, width_n)
    odd_mask = ((total_n[None, :] - wavenum[:, None]) % 2 == 1)[:, None, :]
    even_part = jnp.where(odd_mask, jnp.zeros_like(spectral), spectral)
    odd_part = jnp.where(odd_mask, spectral, jnp.zeros_like(spectral))
    stacked = jnp.concatenate([even_part, odd_part], axis=1)
    halves = jnp.einsum("scn,snj->scj", stacked, legendre, preferred_element_type=jnp.float32)
    even_sum = halves[:, : 2 * level_count]
    odd_sum = halves[:, 2 * level_count :]
    north = (even_sum + odd_sum).astype(jnp.bfloat16)
    south = (even_sum - odd_sum).astype(jnp.bfloat16)
    full = jnp.concatenate([north, jnp.flip(south, axis=2)], axis=2).reshape(
        slot_count, 2, level_count, lat_count
    )
    summed = (
        lax.psum_scatter(full, "lev", scatter_dimension=2, tiled=True)
        .astype(jnp.float32)
        .astype(jnp.bfloat16)
    )
    by_row = jnp.take(summed, lat_of_row, axis=3)
    fourier = lax.all_to_all(by_row, "ma", split_axis=3, concat_axis=0, tiled=True)
    dft_table = build_table(wave_of_slot, NLON)
    pattern = jnp.einsum("srlk,srx->lkx", fourier, dft_table, preferred_element_type=jnp.float32)
    return (new_state, pattern.astype(jnp.bfloat16))


def solution(mesh):
    return jax.shard_map(
        body,
        mesh=mesh,
        in_specs=(
            P("ma", None, None, "lev"),
            P("ma", None, None, "lev"),
            P(),
            P("lev"),
            P("ma", "lev", None),
            P(),
            P(),
        ),
        out_specs=(P("ma", None, None, "lev"), P("lev", "ma", None)),
        check_vma=False,
    )
```

profile of v0, /device:TPU:1, one launch (start us, length us, event | category | flops | bytes accessed | tf_op | source)
XLA Modules:
  0.0 285.0 jit_solution(6675548392480374004)
XLA Ops:
  7.2 0.0 reduce-scatter.2.cloned.1.call-start
  7.2 0.8 dynamic_slice.3
  8.0 0.1 fusion.14
  8.1 8.3 %fusion.19 = (bf16[80,2,32,160]{3,2,1,0:T(8,128)(2,1)}, f32[80,2,32,160]{3,2,1,0:T(8,128)}) fusion(bf16[80,2,32,160]{3,2,1,0:T(8,128)(2,1)} %param.8, f32[160]{0:T(256)} %param.10, f32[80,2,32,160]{3,2,1,0:T(8,128)} %param.7, f32[32]{0:T(128)} %param.9, pred[80,160]{1,0:T(8,128)(4,1)S(1)} %get-tuple-element.13), kind=kLoop, calls=%fused_computation.44 | loop fusion | flops 4915200 | bytes 9843968 | tf_op jit(solution)/shard_map/convert_element_type | solution.py:33
  16.4 3.5 %copy.15 = bf16[80,64,160]{1,2,0:T(8,128)(2,1)S(1)} copy(bf16[80,64,160]{2,1,0:T(8,128)(2,1)} %bitcast.29) | data formatting | bytes 3276800 | tf_op jit(solution)/shard_map/reshape | solution.py:33
  19.9 5.1 %broadcast_select_fusion.1 = (bf16[80,64,160]{1,2,0:T(8,128)(2,1)}, bf16[80,64,160]{1,2,0:T(8,128)(2,1)}) fusion(bf16[80,64,160]{1,2,0:T(8,128)(2,1)S(1)} %copy.15, pred[80,160]{1,0:T(8,128)(4,1)S(1)} %get-tuple-element.12), kind=kLoop, calls=%fused_computation.25 | loop fusion | flops 1638400 | bytes 4928000 | tf_op jit(solution)/shard_map/jit(_where)/select_n | solution.py:35
  25.1 15.9 %fusion.10 = f32[80,128,640]{2,1,0:T(8,128)} fusion(bf16[80,160,640]{2,1,0:T(8,128)(2,1)} %param.11, bf16[80,64,160]{1,2,0:T(8,128)(2,1)} %get-tuple-element.7, bf16[80,64,160]{1,2,0:T(8,128)(2,1)} %get-tuple-element.6), kind=kOutput, calls=%fused_computation.20 | convolution fusion | flops 2103705600 | bytes 45875200 | tf_op jit(solution)/shard_map/scn,snj->scj/dot_general | solution.py:38
  40.9 13.4 %add_convert_fusion = (bf16[80,64,640]{2,1,0:T(8,128)(2,1)}, bf16[80,64,640]{2,1,0:T(8,128)(2,1)}) fusion(f32[80,128,640]{2,1,0:T(8,128)} %fusion.10), kind=kLoop, calls=%fused_computation.15 | loop fusion | flops 13107200 | bytes 39321600 | tf_op jit(solution)/shard_map/convert_element_type | solution.py:41
  54.3 16.6 %rev.4 = bf16[80,64,640]{2,1,0:T(8,128)(2,1)} reverse(bf16[80,64,640]{2,1,0:T(8,128)(2,1)} %get-tuple-element.5), dimensions={2} | reverse | bytes 13107200 | tf_op jit(solution)/shard_map/jit(_flip)/rev | solution.py:43
  71.0 6.5 %pad_maximum_fusion = bf16[80,64,1280]{2,1,0:T(8,128)(2,1)S(1)} fusion(bf16[80,64,640]{2,1,0:T(8,128)(2,1)} %rev.4, bf16[80,64,640]{2,1,0:T(8,128)(2,1)} %get-tuple-element.4), kind=kLoop, calls=%fused_computation.4 | loop fusion | flops 26214400 | bytes 26214400 | tf_op jit(solution)/shard_map/concatenate | solution.py:43
  77.5 21.9 %copy.17 = bf16[80,2,32,1280]{3,0,1,2:T(8,128)(2,1)} copy(bf16[80,2,32,1280]{3,2,1,0:T(8,128)(2,1)S(1)} %bitcast.26) | data formatting | bytes 26214400 | tf_op jit(solution)/shard_map/reshape | solution.py:43
  99.4 0.0 reduce-scatter.2.cloned.1.call-update
  99.4 0.7 copy-done
  100.1 0.0 copy-done.1
  100.1 77.1 %reduce-scatter.2.cloned.1.call-done = bf16[80,2,4,1280]{3,0,1,2:T(8,128)(2,1)} async-done(((bf16[80,2,32,1280]{3,0,1,2:T(8,128)(2,1)}), bf16[80,2,4,1280]{3,0,1,2:T(8,128)(2,1)}) %reduce-scatter.2.cloned.1.call-update) | async-done | bytes 1638416 | tf_op jit(solution)/shard_map/reduce_scatter | solution.py:47
  177.2 5.0 %copy.18 = bf16[80,2,4,1280]{0,2,3,1:T(4,128)(2,1)} copy(bf16[80,2,4,1280]{3,0,1,2:T(8,128)(2,1)} %reduce-scatter.2.cloned.1.call-done) | data formatting | bytes 3276800 | tf_op jit(solution)/shard_map/reduce_scatter | solution.py:47
  182.2 9.6 %gather_fusion = bf16[1280,80,2,4]{1,3,2,0:T(4,128)(2,1)S(1)} fusion(bf16[80,2,4,1280]{0,2,3,1:T(4,128)(2,1)} %copy.18, s32[2048]{0:T(1024)S(1)} %pad_clamp_fusion), kind=kCustom, calls=%fused_computation | custom fusion | bytes 3281920 | tf_op jit(solution)/shard_map/jit(_take)/gather | solution.py:51
  191.8 5.8 %select_bitcast_fusion = bf16[80,2,4,1280]{0,2,1,3:T(4,128)(2,1)} fusion(bf16[1280,80,2,4]{1,3,2,0:T(4,128)(2,1)S(1)} %gather_fusion, pred[1280]{0:T(1024)(128)(4,1)S(1)} %compare_and_fusion), kind=kLoop, calls=%fused_computation.27 | loop fusion | flops 819200 | bytes 3278080 | tf_op jit(solution)/shard_map/jit(_take)/select_n | solution.py:51
  197.6 6.5 %all-to-all-start = ((bf16[80,2,4,1280]{0,2,1,3:T(4,128)(2,1)}), bf16[80,2,4,1280]{0,2,1,3:T(4,128)(2,1)S(1)}, u32[]{:S(2)}, u32[]{:S(2)}) async-start(bf16[80,2,4,1280]{0,2,1,3:T(4,128)(2,1)} %select_bitcast_fusion), calls=%async_computation.1 | async-start | bytes 5242880 | tf_op jit(solution)/shard_map/all_to_all | solution.py:52
  204.2 58.1 %multiply_convert_fusion.1 = (bf16[1280,1,2560]{2,0,1:T(8,128)(2,1)}, bf16[1280,1,2560]{2,0,1:T(8,128)(2,1)}) fusion(s32[1280]{0:T(1024)S(1)} %copy-done.1, f32[1280]{0:T(1024)S(1)} %get-tuple-element.10, f32[1280]{0:T(1024)S(1)} %get-tuple-element.11), kind=kLoop, calls=%fused_computation.10 | loop fusion | flops 42598400 | bytes 13122560 | tf_op jit(solution)/shard_map/convert
  262.3 0.0 all-to-all-done
  262.3 3.1 %copy.22 = bf16[80,2,4,16,80]{0,3,4,1,2:T(8,128)(2,1)} copy(bf16[80,2,4,16,80]{0,2,1,4,3:T(4,128)(2,1)S(1)} %bitcast.27) | data formatting | bytes 3276800 | tf_op jit(solution)/shard_map/all_to_all | solution.py:52
  265.4 4.3 %all_to_all.16 = bf16[1280,2,4,80]{0,3,1,2:T(8,128)(2,1)S(1)} reshape(bf16[16,80,2,4,80]{1,0,4,2,3:T(8,128)(2,1)} %bitcast.28) | data formatting | bytes 3276800 | tf_op jit(solution)/shard_map/all_to_all | solution.py:52
  269.7 8.4 %fusion.9 = bf16[4,80,2560]{2,1,0:T(8,128)(2,1)} fusion(bf16[1280,2,4,80]{0,3,1,2:T(8,128)(2,1)S(1)} %all_to_all.16, bf16[1280,1,2560]{2,0,1:T(8,128)(2,1)} %get-tuple-element.9, bf16[1280,1,2560]{2,0,1:T(8,128)(2,1)} %get-tuple-element.8), kind=kOutput, calls=%fused_computation.19 | convolution fusion | flops 4201676800 | bytes 16384000 | tf_op jit(solution)/shard_map/srlk,srx->lkx/dot_general | solution.py:54
  (7 shorter events, 0.0 us)
Async XLA Ops:
  7.2 170.0 %reduce-scatter.2.cloned.1.call-start = ((), (), s32[]{:S(2)}) async-start(), calls=%async_computation.2 | async-start | bytes 14745600 | tf_op jit(solution)/shard_map/reduce_scatter | solution.py:47
  99.4 0.7 copy-start
  99.4 0.7 copy-start.1
  197.6 64.7 %all-to-all-start = ((bf16[80,2,4,1280]{0,2,1,3:T(4,128)(2,1)}), bf16[80,2,4,1280]{0,2,1,3:T(4,128)(2,1)S(1)}, u32[]{:S(2)}, u32[]{:S(2)}) async-start(bf16[80,2,4,1280]{0,2,1,3:T(4,128)(2,1)} %select_bitcast_fusion), calls=%async_computation.1 | async-start | bytes 5242880 | tf_op jit(solution)/shard_map/all_to_all | solution.py:52
Sparse Core Ops, SparseCore 0:
  99.5 77.6 reduce-scatter.1
where the time goes:
time: 286 us; the launch traced here: 285 us
  other arithmetic  97.4 us (34%)
  waiting for transfers between devices  77.1 us (27%)
  local copies, waits for them, and re-layouts  65.5 us (23%)
  matrix products  24.3 us (8%)
  between operations  14.1 us (5%)
  starting transfers between devices  6.57 us (2%)
    reduce_scatter x1, waiting for transfers between devices, body(): lax.psum_scatter(full, 'lev', scatter_dimension=2, tiled=True)  77.1 us
    another operation x1, other arithmetic  58.1 us
    reshape x1, local copies, waits for them, and re-layouts, body(): jnp.concatenate([north, jnp.flip(south, axis=2)], axis=2)  21.9 us
    rev x1, local copies, waits for them, and re-layouts, body(): jnp.flip(south, axis=2)  16.6 us
    dot_general x1, matrix products, body(): jnp.einsum('scn,snj->scj', stacked, legendre, preferred_element_type=jnp....  15.9 us
    convert_element_type x1, other arithmetic, body(): north = (even_sum + odd_sum).astype(jnp.bfloat16)  13.4 us
    gather x1, local copies, waits for them, and re-layouts, body(): by_row = jnp.take(summed, lat_of_row, axis=3)  9.63 us
    dot_general x1, matrix products, body(): jnp.einsum('srlk,srx->lkx', fourier, dft_table, preferred_element_type=jn...  8.4 us
  transfers between devices with their start and end apart: 2, of which 1 were waited for; matrix products, arithmetic and copies ran while one was open for 20% of the time, Pallas kernels for 0%

commit v1 on v0

v1 whole, which is shorter than its diff:
```python
import functools
import math

import jax
import jax.numpy as jnp
from jax import lax
from jax.experimental import pallas as pl
from jax.experimental.pallas import tpu as pltpu
from jax.sharding import PartitionSpec as P

NLON = 2560
S = 16
RP = 128
MESH = pl.DeviceIdType.MESH
F32 = jnp.float32
BF16 = jnp.bfloat16


def cos_of(v):
    turns = jnp.round(v * F32(1.0 / NLON))
    y = (v - turns * F32(NLON)) * F32(2.0 * math.pi / NLON)
    y2 = y * y
    acc = jnp.full_like(y2, 1.0 / math.factorial(16))
    for k in range(7, -1, -1):
        acc = acc * y2 + F32((-1.0) ** k / math.factorial(2 * k))
    return acc


def column_of(row):
    n = row.shape[1]
    eye = lax.broadcasted_iota(jnp.int32, (n, n), 0) == lax.broadcasted_iota(jnp.int32, (n, n), 1)
    return jnp.sum(jnp.where(eye, jnp.broadcast_to(row, (n, n)), F32(0.0)), axis=1, keepdims=True)


def transform_kernel(
    wave_s, wave_v, lat_v, decay_v, amp_v, st_h, nz_h, lg_h,
    f_out, t_out,
    stb, nzb, lgb, hv, pr, u1, ud, u2, d1, dd, d2, xf, xb, g, gb, tb, mcol,
    ld_sem, dd_s, dd_r, ring_s, ring_r, a2a_s, a2a_r, t_sem,
):
    zn, ns, rows, jn = hv.shape
    ma_n = gb.shape[2]
    nc = ns // S
    levels = stb.shape[3]
    wn = stb.shape[4]
    h = S // 2
    q = S // 4
    me_ma = lax.axis_index("ma")
    me_lev = lax.axis_index("lev")
    z = me_lev // 2
    core = me_lev % 2
    partner = z * 2 + 1 - core
    zu = lax.rem(z + 1, zn)
    zd = lax.rem(z + zn - 1, zn)
    zo = lax.rem(z + 2, zn)
    up = zu * 2 + core
    down = zd * 2 + core

    def load(c):
        b = c % 2
        return [
            pltpu.make_async_copy(st_h.at[pl.ds(c * S, S)], stb.at[b], ld_sem.at[b, 0]),
            pltpu.make_async_copy(nz_h.at[pl.ds(c * S, S)], nzb.at[b], ld_sem.at[b, 1]),
            pltpu.make_async_copy(lg_h.at[pl.ds(c * S, S)], lgb.at[b], ld_sem.at[b, 2]),
        ]

    for c in range(min(2, nc)):
        for cp in load(c):
            cp.start()

    barrier = pltpu.get_barrier_semaphore()
    for lev in (partner, up, down):
        pl.semaphore_signal(barrier, inc=1, device_id={"lev": lev}, device_id_type=MESH)

    def greet(o, carry):
        peer = lax.rem(me_ma + o, ma_n)
        pl.semaphore_signal(barrier, inc=1, device_id={"ma": peer}, device_id_type=MESH)
        pl.semaphore_signal(
            barrier, inc=1, device_id={"ma": peer, "lev": partner}, device_id_type=MESH
        )
        return carry

    lax.fori_loop(1, ma_n, greet, 0)

    dec = jnp.broadcast_to(column_of(decay_v[...]), (levels, wn))
    amp = amp_v[...]
    n_at = me_lev * wn + lax.broadcasted_iota(jnp.int32, (1, 1, wn), 2)
    mcol[...] = jnp.transpose(jnp.broadcast_to(wave_v[...].astype(F32), (8, wave_v.shape[1])))

    def compute(c):
        b = c % 2

        def slot(i, carry):
            m = wave_s[me_ma * ns + c * S + i]
            x = dec[None] * stb[b, i] + amp[None] * nzb[b, i].astype(F32)
            x = jnp.where(n_at >= m, x, F32(0.0)).reshape(2, zn, 8, wn)
            odd = (((n_at - m) & 1) == 1).reshape(1, 1, 1, wn)
            even_part = jnp.where(odd, F32(0.0), x)
            odd_part = jnp.where(odd, x, F32(0.0))
            lhs = jnp.concatenate([even_part, odd_part], axis=2).astype(BF16)
            lhs = lhs.reshape(2 * zn * 16, wn)
            out = jnp.dot(lhs, lgb[b, i], preferred_element_type=F32).astype(BF16)
            for p in range(2):
                for t in range(zn):
                    at = (p * zn + t) * 16
                    hv[t, c * S + i, p * 16 : (p + 1) * 16, :] = out[at : at + 16]
            return carry

        lax.fori_loop(0, S, slot, 0)

    def swap(c):
        return pltpu.make_async_remote_copy(
            src_ref=hv.at[:, pl.ds(c * S + (1 - core) * h, h)],
            dst_ref=pr.at[:, pl.ds(c * h, h)],
            send_sem=dd_s.at[c],
            recv_sem=dd_r.at[c],
            device_id={"lev": partner},
            device_id_type=MESH,
        )

    def hop(c, kind):
        up_to = kind < 3
        box = (u1, ud, u2, d1, dd, d2)[kind]
        plane = (zo, zu, zu, zo, zd, zd)[kind]
        half = (0, 1, 0, 1, 0, 1)[kind]
        return pltpu.make_async_remote_copy(
            src_ref=pr.at[plane, pl.ds(c * h + half * q, q)],
            dst_ref=box.at[pl.ds(c * q, q)],
            send_sem=ring_s.at[c, kind],
            recv_sem=ring_r.at[c, kind],
            device_id={"lev": up if up_to else down},
            device_id_type=MESH,
        )

    def merge(c, plane, first, count, more=None):
        def one(i, carry):
            at = c * h + first + i
            total = hv[plane, c * S + core * h + first + i].astype(F32) + pr[plane, at].astype(F32)
            if more is not None:
                total = total + more[c * q + i].astype(F32)
            pr[plane, at] = total.astype(BF16)
            return carry

        lax.fori_loop(0, count, one, 0)

    def far(c):
        swap(c).wait_recv()
        merge(c, zo, 0, h)
        hop(c, 0).start()
        hop(c, 3).start()

    def near(c):
        merge(c, zu, q, q)
        hop(c, 1).start()
        merge(c, zd, 0, q)
        hop(c, 4).start()

    def relay(c):
        hop(c, 0).wait_recv()
        merge(c, zu, 0, q, u1)
        hop(c, 2).start()
        hop(c, 3).wait_recv()
        merge(c, zd, q, q, d1)
        hop(c, 5).start()

    def finish(c):
        for kind in (1, 2, 4, 5):
            hop(c, kind).wait_recv()
        for half, (r1, r2) in enumerate(((u2, dd), (d2, ud))):

            def one(i, carry):
                at = half * q + i
                total = hv[z, c * S + core * h + at].astype(F32) + pr[z, c * h + at].astype(F32)
                total = total + (r1[c * q + i].astype(F32) + r2[c * q + i].astype(F32))
                for k in range(jn // 128):
                    at_row = pl.ds(pl.multiple_of(at * rows, rows), rows)
                    xf[k, at_row, :] = total[:, k * 128 : (k + 1) * 128]
                return carry

            lax.fori_loop(0, q, one, 0)
        for level in range(8):
            for k in range(jn // 128):
                north = []
                south = []
                for p in range(2):
                    even = xf[k, pl.ds(p * 16 + level, h, stride=rows), :]
                    odd = xf[k, pl.ds(p * 16 + 8 + level, h, stride=rows), :]
                    north.append(even + odd)
                    south.append(even - odd)
                at_row = slice(level * 16, (level + 1) * 16)
                at = k * 128
                xb[at_row, at : at + 128] = jnp.concatenate(north, axis=0).astype(BF16)
                xb[at_row, jn + at : jn + at + 128] = jnp.concatenate(south, axis=0).astype(BF16)

        def pick(m2, carry):
            out = jnp.dot(xb[...], g[m2], preferred_element_type=F32).astype(BF16)
            for tc in range(2):
                for k in range(2):
                    part = out[tc * 64 : (tc + 1) * 64, k * RP : (k + 1) * RP]
                    gb[c, tc, m2 * 2 + k] = part.reshape(4, 16, RP)
            return carry

        lax.fori_loop(0, ma_n // 2, pick, 0)
        place = pl.ds(pl.multiple_of((me_ma * 2 + core) * 16, 16), 16)

        def send(o, tc_flip):
            peer = lax.rem(me_ma + o, ma_n)
            tc = lax.rem(core + tc_flip, 2)
            pltpu.make_async_remote_copy(
                src_ref=gb.at[c, tc, peer],
                dst_ref=f_out.at[c, :, place, :],
                send_sem=a2a_s,
                recv_sem=a2a_r,
                device_id={"ma": peer, "lev": z * 2 + tc},
                device_id_type=MESH,
            ).start()

        def send_both(o, carry):
            send(o, 0)
            send(o, 1)
            return carry

        send(0, 1)
        lax.fori_loop(1, ma_n, send_both, 0)
        pltpu.make_async_copy(gb.at[c, core, me_ma], f_out.at[c, :, place, :], a2a_r).start()

    def selection():
        step = 128
        lane = (2 * RP,)

        def one(m2, carry):
            lat = lat_v[m2]
            for r0 in range(0, 2 * jn, step):
                k = r0 + lax.broadcasted_iota(jnp.int32, (step,) + lane, 0)
                k = k if r0 < jn else 3 * jn - 1 - k
                g[m2, r0 : r0 + step, :] = jnp.where(lat == k, F32(1.0), F32(0.0)).astype(BF16)
            return carry

        lax.fori_loop(0, ma_n // 2, one, 0)

    groups = tb.shape[0] // 16
    per = groups // nc

    def table(c):
        def one(i, carry):
            block = c * per + i
            src = (block % (2 * ma_n)) // 2
            first = src * ns + (block // (2 * ma_n)) * S + (block % 2) * h
            m = mcol[pl.ds(pl.multiple_of(first, 8), 8), 0:1]
            x = lax.broadcasted_iota(jnp.int32, (8, tb.shape[1]), 1).astype(F32)
            v = jnp.broadcast_to(m, (8, tb.shape[1])) * x
            w = jnp.broadcast_to(jnp.where(m == F32(0.0), F32(1.0), F32(2.0)), v.shape)
            both = jnp.concatenate([w * cos_of(v), w * cos_of(v + F32(NLON // 4))], axis=0)
            tb[pl.ds(pl.multiple_of(block * 16, 16), 16), :] = both.astype(BF16)
            return carry

        lax.fori_loop(0, per, one, 0)
        store_table(c).start()

    def store_table(c):
        part = pl.ds(c * per * 16, per * 16)
        return pltpu.make_async_copy(tb.at[part], t_out.at[part], t_sem.at[c])

    def stage(c):
        for cp in load(c):
            cp.wait()
        compute(c)
        if c + 2 < nc:
            for cp in load(c + 2):
                cp.start()
        if c == 0:
            pl.semaphore_wait(barrier, 3 + 2 * (ma_n - 1))
        swap(c).start()

    stage(0)
    stage(1)
    far(0)
    far(1)
    near(0)
    for c in range(2, nc):
        stage(c)
        if c < nc - 1:
            relay(c - 2)
            far(c)
            near(c - 1)
    selection()
    last = nc - 1
    if nc > 2:
        relay(last - 2)
        far(last)
        near(last - 1)
        finish(0)
        table(0)
        for c in range(1, nc - 1):
            if c < nc - 2:
                finish(c)
            table(c)
            if c == nc - 3:
                relay(last - 1)
                near(last)
        if nc == 3:
            relay(last - 1)
            near(last)
        table(nc - 1)
        relay(last)
        finish(nc - 2)
        finish(nc - 1)
    else:
        relay(0)
        near(1)
        table(0)
        relay(1)
        table(1)
        finish(0)
        finish(1)

    for c in range(nc):
        swap(c).wait_send()
        for kind in range(6):
            hop(c, kind).wait_send()
        store_table(c).wait()
    pltpu.make_async_copy(f_out, f_out, a2a_r).wait()
    sent = gb_flat(gb, nc * (2 * ma_n - 1))
    pltpu.make_async_copy(sent, sent, a2a_s).wait()


def gb_flat(gb, count):
    flat = gb.reshape(gb.shape[0] * gb.shape[1] * gb.shape[2], 4, 16, RP)
    return flat.at[pl.ds(0, count)]


def grid_kernel(wave_s, f, sign, t, st, nz, decay_v, amp_v, new_state, out, lhs):
    step = pl.program_id(0)
    nc, ln, kc, _ = f.shape
    rb = out.shape[1]
    half = out.shape[2] // 2
    xb = t.shape[1]

    @pl.when(step == 0)
    def _():
        for c in range(nc):
            for level in range(ln):
                block = jnp.transpose(f[c, level])[:rb]
                at = slice(c * kc, (c + 1) * kc)
                lhs[level * rb : (level + 1) * rb, at] = block
                lhs[(ln + level) * rb : (ln + level + 1) * rb, at] = block * sign[:, at]

    levels = st.shape[2]
    wn = st.shape[3]
    dec = jnp.broadcast_to(column_of(decay_v[...]), (levels, wn))
    amp = amp_v[...]
    n_at = lax.axis_index("lev") * wn + lax.broadcasted_iota(jnp.int32, (1, 1, wn), 2)
    first = lax.axis_index("ma") * (st.shape[0] * pl.num_programs(0)) + step * st.shape[0]

    def slot(i, carry):
        m = wave_s[first + i]
        x = dec[None] * st[i] + amp[None] * nz[i].astype(F32)
        new_state[i] = jnp.where(n_at >= m, x, F32(0.0))
        return carry

    lax.fori_loop(0, st.shape[0], slot, 0)
    for k in range(2):
        for level in range(ln):
            r0 = (k * ln + level) * rb
            part = jnp.dot(lhs[r0 : r0 + rb, :], t[...], preferred_element_type=F32)
            at = pl.ds(pl.multiple_of(k * half + step * xb, 128), xb)
            out[level, :, at] = part.astype(BF16)


def body(spectral_state, forcing_noise, decay_rate, amplitude, legendre, wave_of_slot, lat_of_row):
    ns, _, levels, wn = spectral_state.shape
    jn = legendre.shape[2]
    nlat = lat_of_row.shape[0]
    mn = wave_of_slot.shape[0]
    ma_n = mn // ns
    lev_n = lax.axis_size("lev")
    zn = lev_n // 2
    ln = levels // lev_n
    rb = nlat // ma_n
    nc = ns // S
    kn = 2 * mn
    half = NLON // 2
    wave_row = wave_of_slot.reshape(1, mn)
    lat_rows = jnp.pad(lat_of_row.reshape(ma_n, rb), ((0, 0), (0, RP - rb)), constant_values=-1)
    lat_rows = lat_rows.reshape(ma_n // 2, 1, 2 * RP)
    decay_row = decay_rate.reshape(1, levels)
    amp_row = amplitude.reshape(1, wn)
    sign = (1 - 2 * (wave_of_slot % 2)).astype(BF16).reshape(ma_n, nc, 2, 1, S // 2)
    sign = jnp.broadcast_to(sign.transpose(1, 0, 2, 3, 4), (nc, ma_n, 2, 2, S // 2))
    sign = sign.reshape(1, kn)

    smem = pl.BlockSpec(memory_space=pltpu.SMEM)
    vmem = pl.BlockSpec(memory_space=pltpu.VMEM)
    hbm = pl.BlockSpec(memory_space=pl.ANY)
    box = pltpu.VMEM((nc * S // 4, 32, jn), BF16)
    f, t = pl.pallas_call(
        transform_kernel,
        out_shape=(
            jax.ShapeDtypeStruct((nc, ln, ma_n * 2 * 16, RP), BF16),
            jax.ShapeDtypeStruct((kn, half), BF16),
        ),
        in_specs=[smem, vmem, vmem, vmem, vmem, hbm, hbm, hbm],
        out_specs=(hbm, hbm),
        scratch_shapes=[
            pltpu.VMEM((2, S, 2, levels, wn), F32),
            pltpu.VMEM((2, S, 2, levels, wn), BF16),
            pltpu.VMEM((2, S, wn, jn), BF16),
            pltpu.VMEM((zn, ns, 32, jn), BF16),
            pltpu.VMEM((zn, ns // 2, 32, jn), BF16),
            box, box, box, box, box, box,
            pltpu.VMEM((jn // 128, S // 2 * 32, 128), F32),
            pltpu.VMEM((128, 2 * jn), BF16),
            pltpu.VMEM((ma_n // 2, 2 * jn, 2 * RP), BF16),
            pltpu.VMEM((nc, 2, ma_n, 4, 16, RP), BF16),
            pltpu.VMEM((kn, half), BF16),
            pltpu.VMEM((mn, 8), F32),
            pltpu.SemaphoreType.DMA((2, 3)),
            pltpu.SemaphoreType.DMA((nc,)),
            pltpu.SemaphoreType.DMA((nc,)),
            pltpu.SemaphoreType.DMA((nc, 6)),
            pltpu.SemaphoreType.DMA((nc, 6)),
            pltpu.SemaphoreType.DMA,
            pltpu.SemaphoreType.DMA,
            pltpu.SemaphoreType.DMA((nc,)),
        ],
        compiler_params=pltpu.CompilerParams(
            collective_id=0, has_side_effects=True, vmem_limit_bytes=66_000_000
        ),
        name="transform",
    )(wave_of_slot, wave_row, lat_rows, decay_row, amp_row, spectral_state, forcing_noise, legendre)

    steps = nc
    sb = ns // steps
    xb = half // steps
    new_state, pattern = pl.pallas_call(
        grid_kernel,
        grid=(steps,),
        out_shape=(
            jax.ShapeDtypeStruct((ns, 2, levels, wn), F32),
            jax.ShapeDtypeStruct((ln, rb, NLON), BF16),
        ),
        in_specs=[
            smem,
            pl.BlockSpec(f.shape, lambda i: (0, 0, 0, 0)),
            pl.BlockSpec((1, kn), lambda i: (0, 0)),
            pl.BlockSpec((kn, xb), lambda i: (0, i)),
            pl.BlockSpec((sb, 2, levels, wn), lambda i: (i, 0, 0, 0)),
            pl.BlockSpec((sb, 2, levels, wn), lambda i: (i, 0, 0, 0)),
            pl.BlockSpec((1, levels), lambda i: (0, 0)),
            pl.BlockSpec((1, wn), lambda i: (0, 0)),
        ],
        out_specs=(
            pl.BlockSpec((sb, 2, levels, wn), lambda i: (i, 0, 0, 0)),
            pl.BlockSpec((ln, rb, NLON), lambda i: (0, 0, 0)),
        ),
        scratch_shapes=[pltpu.VMEM((2 * ln * rb, kn), BF16)],
        compiler_params=pltpu.CompilerParams(vmem_limit_bytes=60_000_000),
        name="grid_rows",
    )(wave_of_slot, f, sign, t, spectral_state, forcing_noise, decay_row, amp_row)
    return (new_state, pattern)


def solution(mesh):
    return jax.shard_map(
        body,
        mesh=mesh,
        in_specs=(
            P("ma", None, None, "lev"),
            P("ma", None, None, "lev"),
            P(),
            P("lev"),
            P("ma", "lev", None),
            P(),
            P(),
        ),
        out_specs=(P("ma", None, None, "lev"), P("lev", "ma", None)),
        check_vma=False,
    )
```

time: 286 us -> 110 us (0.38)
  Pallas kernels: 0 us -> 105 us
  other arithmetic: 97.4 us -> 0.71 us
  waiting for transfers between devices: 77.1 us -> 0 us
  local copies, waits for them, and re-layouts: 65.5 us -> 3.59 us
  matrix products: 24.3 us -> 0 us
  between operations: 14.1 us -> 0.66 us
  starting transfers between devices: 6.57 us -> 0 us
    pallas_call x0 -> x2, Pallas kernels: none -> 105 us  [the longest x1 88.5 us: body(): pl.pallas_call(transform_kernel, out_shape=(jax.ShapeDtypeStruct((nc, ln,...]
    reduce_scatter x1 -> x0, waiting for transfers between devices: 77.1 us -> none  [body(): lax.psum_scatter(full, 'lev', scatter_dimension=2, tiled=True)]
    another operation x1 -> x0, other arithmetic: 58.1 us -> none
    dot_general x2 -> x0, matrix products: 24.3 us -> none  [the longest x1 15.9 us: body(): jnp.einsum('scn,snj->scj', stacked, legendre, preferred_element_type=jnp....]
    reshape x2 -> x4, local copies, waits for them, and re-layouts: 25.4 us -> 2.9 us  [the longest x1 1.3 us: body(): wave_row = wave_of_slot.reshape(1, mn)]
    convert_element_type x2 -> x1, other arithmetic: 21.7 us -> 0.71 us  [body(): (1 - 2 * (wave_of_slot % 2)).astype(BF16).reshape(ma_n, nc, 2, 1, S // 2)]
    rev x1 -> x0, local copies, waits for them, and re-layouts: 16.6 us -> none  [body(): jnp.flip(south, axis=2)]
    select_n x4 -> x0, other arithmetic: 11 us -> none  [the longest x2 5.83 us: body(): by_row = jnp.take(summed, lat_of_row, axis=3)]
  transfers between devices with their start and end apart: 2 -> 0, of which waited for: 1 -> 0; matrix products, arithmetic and copies ran while one was open for 20% -> 0% of each run, Pallas kernels for 0% -> 0%
where the time goes in v1:
time: 110 us
  Pallas kernels  105 us (95%)
  local copies, waits for them, and re-layouts  3.59 us (3%)
    pallas_call x1, Pallas kernels, body(): pl.pallas_call(transform_kernel, out_shape=(jax.ShapeDtypeStruct((nc, ln,...  88.5 us
    pallas_call x1, Pallas kernels, body(): pl.pallas_call(grid_kernel, grid=(steps,), out_shape=(jax.ShapeDtypeStruc...  16.5 us

profile of v1, /device:TPU:1, one launch (start us, length us, event | category | flops | bytes accessed | tf_op | source)
XLA Modules:
  0.0 110.0 jit_solution(14415007449403512639)
XLA Ops:
  0.6 0.7 fusion.3
  1.3 1.3 %reshape.25.wave_v = s32[1,1280]{1,0:T(1,128)} reshape(s32[1280]{0:T(1024)} %wave_s.3) | data formatting | bytes 10240 | tf_op jit(solution)/shard_map/reshape | solution.py:383
  2.6 0.8 reshape.26
  3.4 0.6 pad.4
  4.0 0.1 reshape.30
  4.2 0.1 broadcast_in_dim.8
  4.2 0.7 reshape.31.sign
  5.0 88.5 %transform.1 = (bf16[5,4,512,128]{3,2,1,0:T(8,128)(2,1)}, bf16[2560,1280]{1,0:T(8,128)(2,1)}) custom-call(s32[1280]{0:T(1024)} %wave_s.3, s32[1,1280]{1,0:T(1,128)} %reshape.25.wave_v, s32[8,1,256]{2,1,0:T(1,128)} %bitcast.7, f32[1,32]{1,0:T(1,128)} %bitcast.10, f32[1,160]{1,0:T(1,128)} %bitcast.8, f32[80,2,32,160]{3,2,1,0:T(8,128)} %st.1, ...), custom_call_target="tpu_custom_call" | custom-call | tf_op jit(solution)/shard_map/transform/pallas_call | solution.py:396
  93.5 16.5 %grid_rows.1 = (f32[80,2,32,160]{3,2,1,0:T(8,128)}, bf16[4,80,2560]{2,1,0:T(8,128)(2,1)}) custom-call(s32[1280]{0:T(1024)} %wave_s.3, bf16[5,4,512,128]{3,2,1,0:T(8,128)(2,1)} %get-tuple-element.4.f, bf16[1,2560]{1,0:T(2,128)(2,1)} %reshape.31.sign, bf16[2560,1280]{1,0:T(8,128)(2,1)} %get-tuple-element.5.t, f32[80,2,32,160]{3,2,1,0:T(8,128)} %st.1, ...), custom_call_target="tpu_custom_call" | custom-call | tf_op jit(solution)/shard_map/grid_rows/pallas_call | solution.py:435
  (1 shorter events, 0.0 us)

commit v2 on v1

v2 whole, which is shorter than its diff:
```python
import math

import jax
import jax.numpy as jnp
from jax import lax
from jax.experimental import pallas as pl
from jax.experimental.pallas import tpu as pltpu
from jax.sharding import PartitionSpec as P

NLON = 2560
S = 16
H = S // 2
Q = S // 4
DEPTH = 4
RP = 128
BLOCKS = 5
MESH = pl.DeviceIdType.MESH
F32 = jnp.float32
BF16 = jnp.bfloat16


def cos_of(v):
    turns = jnp.round(v * F32(1.0 / NLON))
    y = (v - turns * F32(NLON)) * F32(2.0 * math.pi / NLON)
    y2 = y * y
    acc = jnp.full_like(y2, 1.0 / math.factorial(16))
    for k in range(7, -1, -1):
        acc = acc * y2 + F32((-1.0) ** k / math.factorial(2 * k))
    return acc


def column_of(row):
    n = row.shape[1]
    eye = lax.broadcasted_iota(jnp.int32, (n, n), 0) == lax.broadcasted_iota(jnp.int32, (n, n), 1)
    return jnp.sum(jnp.where(eye, jnp.broadcast_to(row, (n, n)), F32(0.0)), axis=1, keepdims=True)


def signed_rows(rows, sign, lhs):
    m = lhs.shape[0] // 2
    block = jnp.transpose(rows)[:m]
    flip = jnp.transpose(sign)
    flip = jnp.concatenate([flip] * (-(-m // RP)), axis=0)[:m]
    lhs[0:m, :] = block
    lhs[m:, :] = block * flip


def transform_kernel(
    wave_s, wave_v, lat_v, decay_v, amp_v, st_h, nz_h, lg_h,
    f_out, t_out, acc_out,
    stb, nzb, lgb, hv, pr, u1, ud, u2, d1, dd, d2, xf, xb, g, gb, fb, tb, mcol, latp, acc, lhs,
    ld_sem, swap_s, swap_r, ring_s, ring_r, a2a_s, a2a_r, out_sem,
):
    zn, ns, rows, jn = hv.shape
    ma_n = gb.shape[2]
    nc = ns // S
    last = nc - 1
    levels = stb.shape[4]
    wn = stb.shape[5]
    mn = wave_v.shape[0]
    rb = lat_v.shape[0] // ma_n
    ln = acc.shape[0] // (2 * rb)
    half = acc.shape[1]
    kc = fb.shape[1]
    me_ma = lax.axis_index("ma")
    me_lev = lax.axis_index("lev")
    z = me_lev // 2
    core = me_lev % 2
    partner = z * 2 + 1 - core
    zu = lax.rem(z + 1, zn)
    zd = lax.rem(z + zn - 1, zn)
    zo = lax.rem(z + 2, zn)
    up = zu * 2 + core
    down = zd * 2 + core

    def load(u):
        b = u % DEPTH
        return [
            pltpu.make_async_copy(lg_h.at[u // 2, :, u % 2], lgb.at[b], ld_sem.at[b, 2]),
            pltpu.make_async_copy(st_h.at[u // 2, :, u % 2], stb.at[b], ld_sem.at[b, 0]),
            pltpu.make_async_copy(nz_h.at[u // 2, :, u % 2], nzb.at[b], ld_sem.at[b, 1]),
        ]

    barrier = pltpu.get_barrier_semaphore()
    for lev in (partner, up, down):
        pl.semaphore_signal(barrier, inc=1, device_id={"lev": lev}, device_id_type=MESH)

    def greet(o, carry):
        peer = lax.rem(me_ma + o, ma_n)
        pl.semaphore_signal(barrier, inc=1, device_id={"ma": peer}, device_id_type=MESH)
        pl.semaphore_signal(
            barrier, inc=1, device_id={"ma": peer, "lev": partner}, device_id_type=MESH
        )
        return carry

    for u in range(DEPTH):
        for cp in load(u):
            cp.start()
    lax.fori_loop(1, ma_n, greet, 0)

    dec = jnp.broadcast_to(column_of(decay_v[...].reshape(1, levels)), (levels, wn))
    amp = amp_v[...].reshape(1, wn)
    n_at = me_lev * wn + lax.broadcasted_iota(jnp.int32, (1, 1, wn), 2)

    def compute(u):
        b = u % DEPTH

        def slot(i, carry):
            side = i // Q
            at_slot = (u // 2) * S + side * H + (u % 2) * Q + i % Q
            m = wave_s[me_ma * ns + at_slot]
            x = dec[None] * stb[b, side, i % Q] + amp[None] * nzb[b, side, i % Q].astype(F32)
            x = jnp.where(n_at >= m, x, F32(0.0)).reshape(2, zn, 8, wn)
            odd = (((n_at - m) & 1) == 1).reshape(1, 1, 1, wn)
            even_part = jnp.where(odd, F32(0.0), x)
            odd_part = jnp.where(odd, x, F32(0.0))
            left = jnp.concatenate([even_part, odd_part], axis=2).astype(BF16)
            left = left.reshape(2 * zn * 16, wn)
            out = jnp.dot(left, lgb[b, side, i % Q], preferred_element_type=F32).astype(BF16)
            for p in range(2):
                for t in range(zn):
                    at = (p * zn + t) * 16
                    hv[t, at_slot, p * 16 : (p + 1) * 16, :] = out[at : at + 16]
            return carry

        lax.fori_loop(0, H, slot, 0)

    def swap(u):
        first = (u % 2) * Q
        return pltpu.make_async_remote_copy(
            src_ref=hv.at[:, pl.ds((u // 2) * S + (1 - core) * H + first, Q)],
            dst_ref=pr.at[:, pl.ds((u // 2) * H + first, Q)],
            send_sem=swap_s.at[u],
            recv_sem=swap_r.at[u],
            device_id={"lev": partner},
            device_id_type=MESH,
        )

    def stage(u):
        for cp in load(u):
            cp.wait()
        compute(u)
        if u + DEPTH < 2 * nc:
            for cp in load(u + DEPTH):
                cp.start()
        if u == 0:
            pl.semaphore_wait(barrier, 3 + 2 * (ma_n - 1))
        swap(u).start()

    def hop(c, kind):
        box = (u1, ud, u2, d1, dd, d2)[kind]
        plane = (zo, zu, zu, zo, zd, zd)[kind]
        part = (0, 1, 0, 1, 0, 1)[kind]
        return pltpu.make_async_remote_copy(
            src_ref=pr.at[plane, pl.ds(c * H + part * Q, Q)],
            dst_ref=box.at[pl.ds(c * Q, Q)],
            send_sem=ring_s.at[c, kind],
            recv_sem=ring_r.at[c, kind],
            device_id={"lev": up if kind < 3 else down},
            device_id_type=MESH,
        )

    def merge(c, kind, more=None):
        plane = (zo, zu, zu, zo, zd, zd)[kind]
        part = (0, 1, 0, 1, 0, 1)[kind]

        def one(i, carry):
            at = c * H + part * Q + i
            own = c * S + core * H + part * Q + i
            total = hv[plane, own].astype(F32) + pr[plane, at].astype(F32)
            if more is not None:
                total = total + more[c * Q + i].astype(F32)
            pr[plane, at] = total.astype(BF16)
            return carry

        lax.fori_loop(0, Q, one, 0)
        hop(c, kind).start()

    def far(c):
        swap(2 * c).wait_recv()
        merge(c, 0)
        if c == 0:
            merge(c, 4)
            stage(2)
        swap(2 * c + 1).wait_recv()
        merge(c, 3)
        if c == 0:
            merge(c, 1)

    def near(c):
        merge(c, 1)
        merge(c, 4)

    def relay(c):
        hop(c, 0).wait_recv()
        merge(c, 2, u1)
        hop(c, 3).wait_recv()
        merge(c, 5, d1)

    place = pl.ds(pl.multiple_of((me_ma * 2 + core) * 16, 16), 16)

    def landing(c):
        return fb.at[c] if c < last else f_out

    def finish(c):
        for kind in (1, 2, 4, 5):
            hop(c, kind).wait_recv()
        for part, (r1, r2) in enumerate(((u2, dd), (d2, ud))):

            def one(i, carry):
                at = part * Q + i
                total = hv[z, c * S + core * H + at].astype(F32) + pr[z, c * H + at].astype(F32)
                total = total + (r1[c * Q + i].astype(F32) + r2[c * Q + i].astype(F32))
                for k in range(jn // 128):
                    at_row = pl.ds(pl.multiple_of(at * rows, rows), rows)
                    xf[k, at_row, :] = total[:, k * 128 : (k + 1) * 128]
                return carry

            lax.fori_loop(0, Q, one, 0)
        for level in range(8):
            for k in range(jn // 128):
                north = []
                south = []
                for p in range(2):
                    even = xf[k, pl.ds(p * 16 + level, H, stride=rows), :]
                    odd = xf[k, pl.ds(p * 16 + 8 + level, H, stride=rows), :]
                    north.append(even + odd)
                    south.append(even - odd)
                at_row = slice(level * 16, (level + 1) * 16)
                at = k * 128
                xb[at_row, at : at + 128] = jnp.concatenate(north, axis=0).astype(BF16)
                xb[at_row, jn + at : jn + at + 128] = jnp.concatenate(south, axis=0).astype(BF16)
        lanes = gb.shape[4]

        def pick(i, carry):
            m2 = lax.rem(me_ma // 2 + i, ma_n // 2)
            out = jnp.dot(xb[...], g[m2], preferred_element_type=F32)
            for k in range(2):
                peer = m2 * 2 + k
                for tc in range(2):
                    parts = [
                        out[(tc * ln + level) * 16 : (tc * ln + level + 1) * 16, k * RP : k * RP + rb]
                        for level in range(ln)
                    ]
                    if lanes > ln * rb:
                        parts.append(jnp.zeros((16, lanes - ln * rb), F32))
                    gb[c, tc, peer] = jnp.concatenate(parts, axis=1).astype(BF16)
            for k in range(2):
                peer = m2 * 2 + k
                for tc in range(2):

                    @pl.when(jnp.logical_or(peer != me_ma, tc != core))
                    def _():
                        pltpu.make_async_remote_copy(
                            src_ref=gb.at[c, tc, peer],
                            dst_ref=landing(c).at[place, :],
                            send_sem=a2a_s,
                            recv_sem=a2a_r.at[c],
                            device_id={"ma": peer, "lev": z * 2 + tc},
                            device_id_type=MESH,
                        ).start()

            return carry

        lax.fori_loop(0, ma_n // 2, pick, 0)
        if c < last:
            landing(c)[place, :] = gb[c, core, me_ma]
        else:
            pltpu.make_async_copy(gb.at[c, core, me_ma], f_out.at[place, :], out_sem.at[2]).start()

    def selection():
        step = 128
        for m2 in range(ma_n // 2):
            latp[m2] = jnp.full((1, 2 * RP), -1, jnp.int32)
            for k in range(2):
                src = (m2 * 2 + k) * rb
                latp[m2, :, k * RP : k * RP + rb] = lat_v[...].reshape(1, ma_n * rb)[:, src : src + rb]

        def one(m2, carry):
            lat = latp[m2]
            for r0 in range(0, 2 * jn, step):
                k = r0 + lax.broadcasted_iota(jnp.int32, (step, 2 * RP), 0)
                k = k if r0 < jn else 3 * jn - 1 - k
                g[m2, r0 : r0 + step, :] = jnp.where(lat == k, F32(1.0), F32(0.0)).astype(BF16)
            return carry

        lax.fori_loop(0, ma_n // 2, one, 0)

    per = 2 * ma_n

    def table(c):
        def one(i, carry):
            block = c * per + i
            first = (i // 2) * ns + c * S + (i % 2) * H
            m = jnp.broadcast_to(mcol[pl.ds(pl.multiple_of(first, 8), 8), 0:1], (8, RP))
            at = pl.ds(pl.multiple_of(block * 16, 16), 16)
            v = m * lax.broadcasted_iota(jnp.int32, (8, RP), 1).astype(F32)
            turn = m * F32(RP)
            quarter = F32(NLON // 4)
            w = jnp.where(m == F32(0.0), F32(1.0), F32(2.0))
            re, im = w * cos_of(v), w * cos_of(v + quarter)
            tre, tim = cos_of(turn), cos_of(turn + quarter)
            for k in range(half // RP):
                if k:
                    re, im = re * tre - im * tim, re * tim + im * tre
                tb[at, k * RP : (k + 1) * RP] = jnp.concatenate([re, im], axis=0).astype(BF16)
            flip = F32(1.0) - F32(2.0) * (m - F32(2.0) * jnp.floor(m * F32(0.5)))
            tb[at, half:] = jnp.concatenate([flip, flip], axis=0).astype(BF16)
            return carry

        lax.fori_loop(0, per, one, 0, unroll=2)

    def send_table():
        return pltpu.make_async_copy(tb.at[pl.ds(last * kc, kc)], t_out, out_sem.at[0])

    def send_acc():
        return pltpu.make_async_copy(acc, acc_out, out_sem.at[1])

    def along(c):
        whole = fb.at[c, pl.ds(0, kc - 16)]
        pltpu.make_async_copy(whole, whole, a2a_r.at[c]).wait()
        at_row = slice(c * kc, (c + 1) * kc)
        signed_rows(fb[c], tb[at_row, half:], lhs)
        width = half // BLOCKS
        for k in range(BLOCKS):
            at = slice(k * width, (k + 1) * width)
            part = jnp.dot(lhs[...], tb[at_row, at], preferred_element_type=F32)
            acc[:, at] = part if c == 0 else acc[:, at] + part

    stage(0)
    stage(1)
    far(0)
    stage(3)
    for u in range(4, min(6, 2 * nc)):
        stage(u)
    far(1)
    relay(0)
    near(1)
    for c in range(2, nc):
        for u in range(2 * c + 2, min(2 * c + 4, 2 * nc)):
            stage(u)
        if c == 2:
            mcol[...] = jnp.transpose(
                jnp.broadcast_to(wave_v[...].reshape(1, mn).astype(F32), (8, mn))
            )
            selection()
        if c >= 3:
            finish(c - 3)
            table(c - 3)
        if c >= 4:
            along(c - 4)
        far(c)
        relay(c - 1)
        near(c)
    table(last - 2)
    table(last - 1)
    table(last)
    send_table().start()
    finish(last - 2)
    along(last - 3)
    relay(last)
    finish(last - 1)
    along(last - 2)
    finish(last)
    along(last - 1)
    send_acc().start()

    for u in range(2 * nc):
        swap(u).wait_send()
    for c in range(nc):
        for kind in range(6):
            hop(c, kind).wait_send()
    send_table().wait()
    send_acc().wait()
    pltpu.make_async_copy(gb.at[last, core, me_ma], f_out.at[place, :], out_sem.at[2]).wait()
    flat = gb.reshape(nc * 2 * ma_n, 16, gb.shape[4]).at[pl.ds(0, nc * (2 * ma_n - 1))]
    pltpu.make_async_copy(flat, flat, a2a_s).wait()
    whole = f_out.at[pl.ds(0, kc - 16)]
    pltpu.make_async_copy(whole, whole, a2a_r.at[last]).wait()


def grid_kernel(wave_s, f, sign, t, acc, st, nz, decay_v, amp_v, new_state, out, lhs):
    step = pl.program_id(0)
    ln, rb, width = out.shape
    half = width // 2
    xb = t.shape[1]

    @pl.when(step == 0)
    def _():
        signed_rows(f[...], sign[...], lhs)

    levels = st.shape[2]
    wn = st.shape[3]
    dec = jnp.broadcast_to(column_of(decay_v[...].reshape(1, levels)), (levels, wn))
    amp = amp_v[...].reshape(1, wn)
    n_at = lax.axis_index("lev") * wn + lax.broadcasted_iota(jnp.int32, (1, 1, wn), 2)
    first = lax.axis_index("ma") * (st.shape[0] * pl.num_programs(0)) + step * st.shape[0]

    part = (acc[...] + jnp.dot(lhs[...], t[...], preferred_element_type=F32)).astype(BF16)
    for k in range(2):
        at = pl.ds(pl.multiple_of(k * half + step * xb, 128), xb)
        for level in range(ln):
            r0 = (k * ln + level) * rb
            out[level, :, at] = part[r0 : r0 + rb]
    for i in range(st.shape[0]):
        m = wave_s[first + i]
        x = dec[None] * st[i] + amp[None] * nz[i].astype(F32)
        new_state[i] = jnp.where(n_at >= m, x, F32(0.0))


def body(spectral_state, forcing_noise, decay_rate, amplitude, legendre, wave_of_slot, lat_of_row):
    ns, _, levels, wn = spectral_state.shape
    jn = legendre.shape[2]
    nlat = lat_of_row.shape[0]
    mn = wave_of_slot.shape[0]
    ma_n = mn // ns
    lev_n = lax.axis_size("lev")
    zn = lev_n // 2
    ln = levels // lev_n
    rb = nlat // ma_n
    nc = ns // S
    kn = 2 * mn
    kc = kn // nc
    half = NLON // 2
    lanes = -(-(ln * rb) // 128) * 128

    smem = pl.BlockSpec(memory_space=pltpu.SMEM)
    vmem = pl.BlockSpec(memory_space=pltpu.VMEM)
    hbm = pl.BlockSpec(memory_space=pl.ANY)
    box = pltpu.VMEM((nc * Q, 32, jn), BF16)
    dma = pltpu.SemaphoreType.DMA
    f, t, acc = pl.pallas_call(
        transform_kernel,
        out_shape=(
            jax.ShapeDtypeStruct((kc, lanes), BF16),
            jax.ShapeDtypeStruct((kc, half + RP), BF16),
            jax.ShapeDtypeStruct((2 * ln * rb, half), F32),
        ),
        in_specs=[smem, vmem, vmem, vmem, vmem, hbm, hbm, hbm],
        out_specs=(hbm, hbm, hbm),
        scratch_shapes=[
            pltpu.VMEM((DEPTH, 2, Q, 2, levels, wn), F32),
            pltpu.VMEM((DEPTH, 2, Q, 2, levels, wn), BF16),
            pltpu.VMEM((DEPTH, 2, Q, wn, jn), BF16),
            pltpu.VMEM((zn, ns, 32, jn), BF16),
            pltpu.VMEM((zn, ns // 2, 32, jn), BF16),
            box, box, box, box, box, box,
            pltpu.VMEM((jn // 128, H * 32, 128), F32),
            pltpu.VMEM((128, 2 * jn), BF16),
            pltpu.VMEM((ma_n // 2, 2 * jn, 2 * RP), BF16),
            pltpu.VMEM((nc, 2, ma_n, 16, lanes), BF16),
            pltpu.VMEM((nc - 1, kc, lanes), BF16),
            pltpu.VMEM((kn, half + RP), BF16),
            pltpu.VMEM((mn, 8), F32),
            pltpu.VMEM((ma_n // 2, 1, 2 * RP), jnp.int32),
            pltpu.VMEM((2 * ln * rb, half), F32),
            pltpu.VMEM((2 * ln * rb, kc), BF16),
            dma((DEPTH, 3)),
            dma((2 * nc,)),
            dma((2 * nc,)),
            dma((nc, 6)),
            dma((nc, 6)),
            dma,
            dma((nc,)),
            dma((3,)),
        ],
        compiler_params=pltpu.CompilerParams(
            collective_id=0, has_side_effects=True, vmem_limit_bytes=66_000_000
        ),
        name="transform",
    )(
        wave_of_slot, wave_of_slot, lat_of_row, decay_rate, amplitude,
        spectral_state.reshape(nc, 2, 2, Q, 2, levels, wn),
        forcing_noise.reshape(nc, 2, 2, Q, 2, levels, wn),
        legendre.reshape(nc, 2, 2, Q, wn, jn),
    )

    sb = ns // BLOCKS
    xb = half // BLOCKS
    new_state, pattern = pl.pallas_call(
        grid_kernel,
        grid=(BLOCKS,),
        out_shape=(
            jax.ShapeDtypeStruct((ns, 2, levels, wn), F32),
            jax.ShapeDtypeStruct((ln, rb, NLON), BF16),
        ),
        in_specs=[
            smem,
            pl.BlockSpec(f.shape, lambda i: (0, 0)),
            pl.BlockSpec((kc, RP), lambda i: (0, half // RP)),
            pl.BlockSpec((kc, xb), lambda i: (0, i)),
            pl.BlockSpec((2 * ln * rb, xb), lambda i: (0, i)),
            pl.BlockSpec((sb, 2, levels, wn), lambda i: (i, 0, 0, 0)),
            pl.BlockSpec((sb, 2, levels, wn), lambda i: (i, 0, 0, 0)),
            vmem,
            vmem,
        ],
        out_specs=(
            pl.BlockSpec((sb, 2, levels, wn), lambda i: (i, 0, 0, 0)),
            pl.BlockSpec((ln, rb, NLON), lambda i: (0, 0, 0)),
        ),
        scratch_shapes=[pltpu.VMEM((2 * ln * rb, kc), BF16)],
        compiler_params=pltpu.CompilerParams(vmem_limit_bytes=60_000_000),
        name="grid_rows",
    )(wave_of_slot, f, t, t, acc, spectral_state, forcing_noise, decay_rate, amplitude)
    return (new_state, pattern)


def solution(mesh):
    return jax.shard_map(
        body,
        mesh=mesh,
        in_specs=(
            P("ma", None, None, "lev"),
            P("ma", None, None, "lev"),
            P(),
            P("lev"),
            P("ma", "lev", None),
            P(),
            P(),
        ),
        out_specs=(P("ma", None, None, "lev"), P("lev", "ma", None)),
        check_vma=False,
    )
```

time: 110 us -> 88.3 us (0.80)
  Pallas kernels: 105 us -> 87.4 us
  local copies, waits for them, and re-layouts: 3.59 us -> 0 us
    pallas_call x2, Pallas kernels: 105 us -> 87.4 us  [the longest x1 77.5 us: body(): pl.pallas_call(transform_kernel, out_shape=(jax.ShapeDtypeStruct((kc, lan...]
    reshape x4 -> x0, local copies, waits for them, and re-layouts: 2.9 us -> none  [the longest x1 1.3 us: body(): wave_row = wave_of_slot.reshape(1, mn)]
where the time goes in v2:
time: 88.3 us; the launch traced here: 88 us
  Pallas kernels  87.4 us (99%)
    pallas_call x1, Pallas kernels, body(): pl.pallas_call(transform_kernel, out_shape=(jax.ShapeDtypeStruct((kc, lan...  77.5 us
    pallas_call x1, Pallas kernels, body(): pl.pallas_call(grid_kernel, grid=(BLOCKS,), out_shape=(jax.ShapeDtypeStru...  9.9 us

profile of v2, /device:TPU:1, one launch (start us, length us, event | category | flops | bytes accessed | tf_op | source)
XLA Modules:
  0.0 88.0 jit_solution(2893763959599286368)
XLA Ops:
  0.6 77.5 %transform.1 = (bf16[512,384]{1,0:T(8,128)(2,1)}, bf16[512,1408]{1,0:T(8,128)(2,1)}, f32[640,1280]{1,0:T(8,128)}) custom-call(s32[1280]{0:T(1024)} %wave_s.3, s32[1280]{0:T(1024)} %wave_s.3, s32[1280]{0:T(1024)} %lat_v.1, f32[32]{0:T(128)} %decay_v.3, f32[160]{0:T(256)} %amp_v.3, f32[5,2,2,4,2,32,160]{6,5,4,3,2,1,0:T(8,128)} %bitcast.3, ...), custom_call_target="tpu_custom_call" | custom-call | tf_op jit(solution)/shard_map/transform/pallas_call | solution.py:431
  78.1 9.9 %grid_rows.1 = (f32[80,2,32,160]{3,2,1,0:T(8,128)}, bf16[4,80,2560]{2,1,0:T(8,128)(2,1)}) custom-call(s32[1280]{0:T(1024)} %wave_s.3, bf16[512,384]{1,0:T(8,128)(2,1)} %get-tuple-element.5.f, bf16[512,1408]{1,0:T(8,128)(2,1)} %get-tuple-element.6.sign.t, bf16[512,1408]{1,0:T(8,128)(2,1)} %get-tuple-element.6.sign.t, f32[640,1280]{1,0:T(8,128)} %get-tuple-element.7.acc, ...), custom_call_target="tpu_custom_call" | custom-call | tf_op jit(solution)/shard_map/grid_rows/pallas_call | solution.py:479

commit v3 on v2

--- a/solution.py
+++ b/solution.py
@@ -45,10 +45,10 @@
 
 
 def transform_kernel(
-    wave_s, wave_v, lat_v, decay_v, amp_v, st_h, nz_h, lg_h,
-    f_out, t_out, acc_out,
-    stb, nzb, lgb, hv, pr, u1, ud, u2, d1, dd, d2, xf, xb, g, gb, fb, tb, mcol, latp, acc, lhs,
-    ld_sem, swap_s, swap_r, ring_s, ring_r, a2a_s, a2a_r, out_sem,
+    wave_h, lat_h, decay_h, amp_h, st_h, nz_h, lg_h,
+    f_out, t_out, acc_out, ns_out,
+    wave_s, wave_v, lat_v, decay_v, amp_v, stb, nzb, nsb, lgb, hv, pr, u1, ud, u2, d1, dd, d2, xf, xb, g, gb, fb, tb, mcol, latp, acc, accb, lhs,
+    small_sem, ns_sem, ld_sem, swap_s, swap_r, ring_s, ring_r, a2a_s, a2a_r, out_sem,
 ):
     zn, ns, rows, jn = hv.shape
     ma_n = gb.shape[2]
@@ -72,13 +72,17 @@
     up = zu * 2 + core
     down = zd * 2 + core
 
-    def load(u):
+    def load(u, k):
         b = u % DEPTH
+        side = (1 - core, core)[k]
         return [
-            pltpu.make_async_copy(lg_h.at[u // 2, :, u % 2], lgb.at[b], ld_sem.at[b, 2]),
-            pltpu.make_async_copy(st_h.at[u // 2, :, u % 2], stb.at[b], ld_sem.at[b, 0]),
-            pltpu.make_async_copy(nz_h.at[u // 2, :, u % 2], nzb.at[b], ld_sem.at[b, 1]),
+            pltpu.make_async_copy(src.at[u // 2, side, u % 2], dst.at[b, k], ld_sem.at[b, k, n])
+            for n, (src, dst) in enumerate(((lg_h, lgb), (st_h, stb), (nz_h, nzb)))
         ]
+
+    def fetch(u):
+        for cp in load(u, 0) + load(u, 1):
+            cp.start()
 
     barrier = pltpu.get_barrier_semaphore()
     for lev in (partner, up, down):
@@ -92,37 +96,51 @@
         )
         return carry
 
-    for u in range(DEPTH):
-        for cp in load(u):
-            cp.start()
+    small = [
+        pltpu.make_async_copy(src, dst, small_sem.at[k])
+        for k, (src, dst) in enumerate(
+            (
+                (wave_h, wave_s),
+                (decay_h, decay_v),
+                (amp_h, amp_v),
+                (wave_h, wave_v),
+                (lat_h, lat_v),
+            )
+        )
+    ]
+    for cp in small[:3] + load(0, 0) + load(0, 1):
+        cp.start()
     lax.fori_loop(1, ma_n, greet, 0)
-
+    for cp in small[:3]:
+        cp.wait()
     dec = jnp.broadcast_to(column_of(decay_v[...].reshape(1, levels)), (levels, wn))
     amp = amp_v[...].reshape(1, wn)
     n_at = me_lev * wn + lax.broadcasted_iota(jnp.int32, (1, 1, wn), 2)
 
-    def compute(u):
+    def compute(u, k):
         b = u % DEPTH
+        side = (1 - core, core)[k]
 
         def slot(i, carry):
-            side = i // Q
-            at_slot = (u // 2) * S + side * H + (u % 2) * Q + i % Q
+            at_slot = (u // 2) * S + side * H + (u % 2) * Q + i
             m = wave_s[me_ma * ns + at_slot]
-            x = dec[None] * stb[b, side, i % Q] + amp[None] * nzb[b, side, i % Q].astype(F32)
-            x = jnp.where(n_at >= m, x, F32(0.0)).reshape(2, zn, 8, wn)
+            x = dec[None] * stb[b, k, i] + amp[None] * nzb[b, k, i].astype(F32)
+            x = jnp.where(n_at >= m, x, F32(0.0))
+            nsb[b, k, i] = x
+            x = x.reshape(2, zn, 8, wn)
             odd = (((n_at - m) & 1) == 1).reshape(1, 1, 1, wn)
             even_part = jnp.where(odd, F32(0.0), x)
             odd_part = jnp.where(odd, x, F32(0.0))
             left = jnp.concatenate([even_part, odd_part], axis=2).astype(BF16)
             left = left.reshape(2 * zn * 16, wn)
-            out = jnp.dot(left, lgb[b, side, i % Q], preferred_element_type=F32).astype(BF16)
+            out = jnp.dot(left, lgb[b, k, i], preferred_element_type=F32).astype(BF16)
             for p in range(2):
                 for t in range(zn):
                     at = (p * zn + t) * 16
                     hv[t, at_slot, p * 16 : (p + 1) * 16, :] = out[at : at + 16]
             return carry
 
-        lax.fori_loop(0, H, slot, 0)
+        lax.fori_loop(0, Q, slot, 0, unroll=2)
 
     def swap(u):
         first = (u % 2) * Q
@@ -135,16 +153,39 @@
             device_id_type=MESH,
         )
 
+    def keep(u):
+        b = u % DEPTH
+        return [
+            pltpu.make_async_copy(
+                nsb.at[b, k], ns_out.at[u // 2, (1 - core, core)[k], u % 2], ns_sem.at[b, k]
+            )
+            for k in range(2)
+        ]
+
     def stage(u):
-        for cp in load(u):
+        for cp in load(u, 0):
             cp.wait()
-        compute(u)
-        if u + DEPTH < 2 * nc:
-            for cp in load(u + DEPTH):
-                cp.start()
+        if u == 0:
+            fetch(1)
+        if u >= DEPTH:
+            for cp in keep(u - DEPTH):
+                cp.wait()
+        compute(u, 0)
         if u == 0:
             pl.semaphore_wait(barrier, 3 + 2 * (ma_n - 1))
         swap(u).start()
+        for cp in load(u, 1):
+            cp.wait()
+        if u == 0:
+            for v in range(2, DEPTH):
+                fetch(v)
+            for cp in small[3:]:
+                cp.start()
+        compute(u, 1)
+        for cp in keep(u):
+            cp.start()
+        if u + DEPTH < 2 * nc:
+            fetch(u + DEPTH)
 
     def hop(c, kind):
         box = (u1, ud, u2, d1, dd, d2)[kind]
@@ -232,7 +273,8 @@
         lanes = gb.shape[4]
 
         def pick(i, carry):
-            m2 = lax.rem(me_ma // 2 + i, ma_n // 2)
+            pairs = ma_n // 2
+            m2 = lax.rem(me_ma // 2 + pairs + pairs // 2 + (2 * (i % 2) - 1) * ((i + 1) // 2), pairs)
             out = jnp.dot(xb[...], g[m2], preferred_element_type=F32)
             for k in range(2):
                 peer = m2 * 2 + k
@@ -313,7 +355,7 @@
         return pltpu.make_async_copy(tb.at[pl.ds(last * kc, kc)], t_out, out_sem.at[0])
 
     def send_acc():
-        return pltpu.make_async_copy(acc, acc_out, out_sem.at[1])
+        return pltpu.make_async_copy(accb, acc_out, out_sem.at[1])
 
     def along(c):
         whole = fb.at[c, pl.ds(0, kc - 16)]
@@ -324,21 +366,25 @@
         for k in range(BLOCKS):
             at = slice(k * width, (k + 1) * width)
             part = jnp.dot(lhs[...], tb[at_row, at], preferred_element_type=F32)
-            acc[:, at] = part if c == 0 else acc[:, at] + part
+            total = part if c == 0 else acc[:, at] + part
+            if c < last - 1:
+                acc[:, at] = total
+            else:
+                accb[:, at] = total.astype(BF16)
 
     stage(0)
     stage(1)
     far(0)
     stage(3)
-    for u in range(4, min(6, 2 * nc)):
-        stage(u)
     far(1)
+    stage(4)
     relay(0)
     near(1)
     for c in range(2, nc):
-        for u in range(2 * c + 2, min(2 * c + 4, 2 * nc)):
-            stage(u)
+        stage(2 * c + 1)
         if c == 2:
+            for cp in small[3:]:
+                cp.wait()
             mcol[...] = jnp.transpose(
                 jnp.broadcast_to(wave_v[...].reshape(1, mn).astype(F32), (8, mn))
             )
@@ -349,6 +395,8 @@
         if c >= 4:
             along(c - 4)
         far(c)
+        if c < last:
+            stage(2 * c + 2)
         relay(c - 1)
         near(c)
     table(last - 2)
@@ -366,6 +414,9 @@
 
     for u in range(2 * nc):
         swap(u).wait_send()
+    for u in range(2 * nc - DEPTH, 2 * nc):
+        for cp in keep(u):
+            cp.wait()
     for c in range(nc):
         for kind in range(6):
             hop(c, kind).wait_send()
@@ -378,33 +429,59 @@
     pltpu.make_async_copy(whole, whole, a2a_r.at[last]).wait()
 
 
-def grid_kernel(wave_s, f, sign, t, acc, st, nz, decay_v, amp_v, new_state, out, lhs):
-    step = pl.program_id(0)
-    ln, rb, width = out.shape
+def grid_kernel(f_h, t_h, acc_h, kept_h, new_h, out_h, f, t, acc, kept, lhs, obuf, in_sem, keep_sem, out_sem):
+    ln, rb, width = out_h.shape
     half = width // 2
-    xb = t.shape[1]
-
-    @pl.when(step == 0)
-    def _():
-        signed_rows(f[...], sign[...], lhs)
-
-    levels = st.shape[2]
-    wn = st.shape[3]
-    dec = jnp.broadcast_to(column_of(decay_v[...].reshape(1, levels)), (levels, wn))
-    amp = amp_v[...].reshape(1, wn)
-    n_at = lax.axis_index("lev") * wn + lax.broadcasted_iota(jnp.int32, (1, 1, wn), 2)
-    first = lax.axis_index("ma") * (st.shape[0] * pl.num_programs(0)) + step * st.shape[0]
-
-    part = (acc[...] + jnp.dot(lhs[...], t[...], preferred_element_type=F32)).astype(BF16)
-    for k in range(2):
-        at = pl.ds(pl.multiple_of(k * half + step * xb, 128), xb)
-        for level in range(ln):
-            r0 = (k * ln + level) * rb
-            out[level, :, at] = part[r0 : r0 + rb]
-    for i in range(st.shape[0]):
-        m = wave_s[first + i]
-        x = dec[None] * st[i] + amp[None] * nz[i].astype(F32)
-        new_state[i] = jnp.where(n_at >= m, x, F32(0.0))
+    xb = half // BLOCKS
+    parts = kept_h.shape[0]
+
+    first = [
+        pltpu.make_async_copy(f_h, f, in_sem.at[0]),
+        pltpu.make_async_copy(t_h, t, in_sem.at[1]),
+        pltpu.make_async_copy(acc_h, acc, in_sem.at[2]),
+    ]
+    take = [
+        pltpu.make_async_copy(kept_h.at[c], kept.at[c], keep_sem.at[0, c]) for c in range(parts)
+    ]
+    give = [
+        pltpu.make_async_copy(kept.at[c], new_h.at[c], keep_sem.at[1, c]) for c in range(parts)
+    ]
+
+    def store(k):
+        return [
+            pltpu.make_async_copy(
+                obuf.at[k, p],
+                out_h.at[:, :, pl.ds(p * half + k * xb, xb)],
+                out_sem.at[k, p],
+            )
+            for p in range(2)
+        ]
+
+    for cp in first[:2] + take[:2] + first[2:] + take[2:]:
+        cp.start()
+    first[0].wait()
+    first[1].wait()
+    signed_rows(f[...], t[:, half:], lhs)
+    first[2].wait()
+    for k in range(max(BLOCKS, parts)):
+        if k < parts:
+            take[k].wait()
+            give[k].start()
+        if k < BLOCKS:
+            at = slice(k * xb, (k + 1) * xb)
+            part = jnp.dot(lhs[...], t[:, at], preferred_element_type=F32)
+            part = (acc[:, at].astype(F32) + part).astype(BF16)
+            for p in range(2):
+                for level in range(ln):
+                    r0 = (p * ln + level) * rb
+                    obuf[k, p, level] = part[r0 : r0 + rb]
+            for cp in store(k):
+                cp.start()
+    for k in range(BLOCKS):
+        for cp in store(k):
+            cp.wait()
+    for cp in give:
+        cp.wait()
 
 
 def body(spectral_state, forcing_noise, decay_rate, amplitude, legendre, wave_of_slot, lat_of_row):
@@ -428,18 +505,25 @@
     hbm = pl.BlockSpec(memory_space=pl.ANY)
     box = pltpu.VMEM((nc * Q, 32, jn), BF16)
     dma = pltpu.SemaphoreType.DMA
-    f, t, acc = pl.pallas_call(
+    f, t, acc, kept = pl.pallas_call(
         transform_kernel,
         out_shape=(
             jax.ShapeDtypeStruct((kc, lanes), BF16),
             jax.ShapeDtypeStruct((kc, half + RP), BF16),
-            jax.ShapeDtypeStruct((2 * ln * rb, half), F32),
+            jax.ShapeDtypeStruct((2 * ln * rb, half), BF16),
+            jax.ShapeDtypeStruct((nc, 2, 2, Q, 2, levels, wn), F32),
         ),
-        in_specs=[smem, vmem, vmem, vmem, vmem, hbm, hbm, hbm],
-        out_specs=(hbm, hbm, hbm),
+        in_specs=[hbm] * 7,
+        out_specs=(hbm,) * 4,
         scratch_shapes=[
+            pltpu.SMEM((mn,), jnp.int32),
+            pltpu.VMEM((mn,), jnp.int32),
+            pltpu.VMEM((nlat,), jnp.int32),
+            pltpu.VMEM((levels,), F32),
+            pltpu.VMEM((wn,), F32),
             pltpu.VMEM((DEPTH, 2, Q, 2, levels, wn), F32),
             pltpu.VMEM((DEPTH, 2, Q, 2, levels, wn), BF16),
+            pltpu.VMEM((DEPTH, 2, Q, 2, levels, wn), F32),
             pltpu.VMEM((DEPTH, 2, Q, wn, jn), BF16),
             pltpu.VMEM((zn, ns, 32, jn), BF16),
             pltpu.VMEM((zn, ns // 2, 32, jn), BF16),
@@ -453,8 +537,11 @@
             pltpu.VMEM((mn, 8), F32),
             pltpu.VMEM((ma_n // 2, 1, 2 * RP), jnp.int32),
             pltpu.VMEM((2 * ln * rb, half), F32),
+            pltpu.VMEM((2 * ln * rb, half), BF16),
             pltpu.VMEM((2 * ln * rb, kc), BF16),
-            dma((DEPTH, 3)),
+            dma((5,)),
+            dma((DEPTH, 2)),
+            dma((DEPTH, 2, 3)),
             dma((2 * nc,)),
             dma((2 * nc,)),
             dma((nc, 6)),
@@ -468,41 +555,36 @@
         ),
         name="transform",
     )(
-        wave_of_slot, wave_of_slot, lat_of_row, decay_rate, amplitude,
+        wave_of_slot, lat_of_row, decay_rate, amplitude,
         spectral_state.reshape(nc, 2, 2, Q, 2, levels, wn),
         forcing_noise.reshape(nc, 2, 2, Q, 2, levels, wn),
         legendre.reshape(nc, 2, 2, Q, wn, jn),
     )
 
-    sb = ns // BLOCKS
     xb = half // BLOCKS
     new_state, pattern = pl.pallas_call(
         grid_kernel,
-        grid=(BLOCKS,),
         out_shape=(
-            jax.ShapeDtypeStruct((ns, 2, levels, wn), F32),
+            jax.ShapeDtypeStruct((nc, S, 2, levels, wn), F32),
             jax.ShapeDtypeStruct((ln, rb, NLON), BF16),
         ),
-        in_specs=[
-            smem,
-            pl.BlockSpec(f.shape, lambda i: (0, 0)),
-            pl.BlockSpec((kc, RP), lambda i: (0, half // RP)),
-            pl.BlockSpec((kc, xb), lambda i: (0, i)),
-            pl.BlockSpec((2 * ln * rb, xb), lambda i: (0, i)),
-            pl.BlockSpec((sb, 2, levels, wn), lambda i: (i, 0, 0, 0)),
-            pl.BlockSpec((sb, 2, levels, wn), lambda i: (i, 0, 0, 0)),
-            vmem,
-            vmem,
+        in_specs=[hbm] * 4,
+        out_specs=(hbm, hbm),
+        scratch_shapes=[
+            pltpu.VMEM((kc, lanes), BF16),
+            pltpu.VMEM((kc, half + RP), BF16),
+            pltpu.VMEM((2 * ln * rb, half), BF16),
+            pltpu.VMEM((nc, S, 2, levels, wn), F32),
+            pltpu.VMEM((2 * ln * rb, kc), BF16),
+            pltpu.VMEM((BLOCKS, 2, ln, rb, xb), BF16),
+            dma((3,)),
+            dma((2, nc)),
+            dma((BLOCKS, 2)),
         ],
-        out_specs=(
-            pl.BlockSpec((sb, 2, levels, wn), lambda i: (i, 0, 0, 0)),
-            pl.BlockSpec((ln, rb, NLON), lambda i: (0, 0, 0)),
-        ),
-        scratch_shapes=[pltpu.VMEM((2 * ln * rb, kc), BF16)],
         compiler_params=pltpu.CompilerParams(vmem_limit_bytes=60_000_000),
         name="grid_rows",
-    )(wave_of_slot, f, t, t, acc, spectral_state, forcing_noise, decay_rate, amplitude)
-    return (new_state, pattern)
+    )(f, t, acc, kept.reshape(nc, S, 2, levels, wn))
+    return (new_state.reshape(ns, 2, levels, wn), pattern)
 
 
 def solution(mesh):

time: 88.3 us -> 83 us (0.940)
  Pallas kernels: 87.4 us -> 82.1 us
    pallas_call x1, Pallas kernels: 9.9 us -> 6.47 us  [body(): pl.pallas_call(grid_kernel, out_shape=(jax.ShapeDtypeStruct((nc, S, 2, le...]
    pallas_call x1, Pallas kernels: 77.5 us -> 75.6 us  [body(): pl.pallas_call(transform_kernel, out_shape=(jax.ShapeDtypeStruct((kc, lan...]
where the time goes in v3:
time: 83 us; the launch traced here: 82.9 us
  Pallas kernels  82.1 us (99%)
    pallas_call x1, Pallas kernels, body(): pl.pallas_call(transform_kernel, out_shape=(jax.ShapeDtypeStruct((kc, lan...  75.6 us
    pallas_call x1, Pallas kernels, body(): pl.pallas_call(grid_kernel, out_shape=(jax.ShapeDtypeStruct((nc, S, 2, le...  6.47 us

profile of v3, /device:TPU:1, one launch (start us, length us, event | category | flops | bytes accessed | tf_op | source)
XLA Modules:
  0.0 82.9 jit_solution(5099119771039986807)
XLA Ops:
  0.6 75.6 %transform.1 = (bf16[512,384]{1,0:T(8,128)(2,1)}, bf16[512,1408]{1,0:T(8,128)(2,1)}, bf16[640,1280]{1,0:T(8,128)(2,1)}, f32[5,2,2,4,2,32,160]{6,5,4,3,2,1,0:T(8,128)}) custom-call(s32[1280]{0:T(1024)} %wave_h.1, s32[1280]{0:T(1024)} %lat_h.1, f32[32]{0:T(128)} %decay_h.1, f32[160]{0:T(256)} %amp_h.1, f32[5,2,2,4,2,32,160]{6,5,4,3,2,1,0:T(8,128)} %bitcast.7, ...), custom_call_target="tpu_custom_call" | custom-call | tf_op jit(solution)/shard_map/transform/pallas_call | solution.py:508
  76.2 6.5 %grid_rows.1 = (f32[5,16,2,32,160]{4,3,2,1,0:T(8,128)}, bf16[4,80,2560]{2,1,0:T(8,128)(2,1)}) custom-call(bf16[512,384]{1,0:T(8,128)(2,1)} %get-tuple-element.8.f_h, bf16[512,1408]{1,0:T(8,128)(2,1)} %get-tuple-element.9.t_h, bf16[640,1280]{1,0:T(8,128)(2,1)} %get-tuple-element.10.acc_h, f32[5,16,2,32,160]{4,3,2,1,0:T(8,128)} %bitcast.6), custom_call_target="tpu_custom_call" | custom-call | tf_op jit(solution)/shard_map/grid_rows/pallas_call | solution.py:565

commit v4 on v3

--- a/solution.py
+++ b/solution.py
@@ -11,7 +11,8 @@
 S = 16
 H = S // 2
 Q = S // 4
-DEPTH = 4
+DEPTH = 3
+ORDER = (0, 1, 2, 3, 8, 4, 5, 9, 6, 7)
 RP = 128
 BLOCKS = 5
 MESH = pl.DeviceIdType.MESH
@@ -47,12 +48,13 @@
 def transform_kernel(
     wave_h, lat_h, decay_h, amp_h, st_h, nz_h, lg_h,
     f_out, t_out, acc_out, ns_out,
-    wave_s, wave_v, lat_v, decay_v, amp_v, stb, nzb, nsb, lgb, hv, pr, u1, ud, u2, d1, dd, d2, xf, xb, g, gb, fb, tb, mcol, latp, acc, accb, lhs,
-    small_sem, ns_sem, ld_sem, swap_s, swap_r, ring_s, ring_r, a2a_s, a2a_r, out_sem,
+    wave_s, wave_v, lat_v, decay_v, amp_v, stb, nzb, nsb, lgb, hv, pr, u1, ud, u2, d1, dd, d2, perm, xn, xb, g, gb, gbs, fb, sa, sbox, tb, mcol, latp, acc, accb, lhs,
+    small_sem, ns_sem, ld_sem, swap_s, swap_r, ring_s, ring_r, a2a_s, a2a_s2, a2a_r, out_sem,
 ):
     zn, ns, rows, jn = hv.shape
     ma_n = gb.shape[2]
     nc = ns // S
+    assert 2 * nc == len(ORDER)
     last = nc - 1
     levels = stb.shape[4]
     wn = stb.shape[5]
@@ -73,7 +75,7 @@
     down = zd * 2 + core
 
     def load(u, k):
-        b = u % DEPTH
+        b = ORDER.index(u) % DEPTH
         side = (1 - core, core)[k]
         return [
             pltpu.make_async_copy(src.at[u // 2, side, u % 2], dst.at[b, k], ld_sem.at[b, k, n])
@@ -118,7 +120,7 @@
     n_at = me_lev * wn + lax.broadcasted_iota(jnp.int32, (1, 1, wn), 2)
 
     def compute(u, k):
-        b = u % DEPTH
+        b = ORDER.index(u) % DEPTH
         side = (1 - core, core)[k]
 
         def slot(i, carry):
@@ -154,7 +156,7 @@
         )
 
     def keep(u):
-        b = u % DEPTH
+        b = ORDER.index(u) % DEPTH
         return [
             pltpu.make_async_copy(
                 nsb.at[b, k], ns_out.at[u // 2, (1 - core, core)[k], u % 2], ns_sem.at[b, k]
@@ -167,8 +169,9 @@
             cp.wait()
         if u == 0:
             fetch(1)
-        if u >= DEPTH:
-            for cp in keep(u - DEPTH):
+        at = ORDER.index(u)
+        if at >= DEPTH:
+            for cp in keep(ORDER[at - DEPTH]):
                 cp.wait()
         compute(u, 0)
         if u == 0:
@@ -177,15 +180,15 @@
         for cp in load(u, 1):
             cp.wait()
         if u == 0:
-            for v in range(2, DEPTH):
+            for v in ORDER[2:DEPTH]:
                 fetch(v)
             for cp in small[3:]:
                 cp.start()
         compute(u, 1)
         for cp in keep(u):
             cp.start()
-        if u + DEPTH < 2 * nc:
-            fetch(u + DEPTH)
+        if at + DEPTH < 2 * nc:
+            fetch(ORDER[at + DEPTH])
 
     def hop(c, kind):
         box = (u1, ud, u2, d1, dd, d2)[kind]
@@ -239,38 +242,18 @@
 
     place = pl.ds(pl.multiple_of((me_ma * 2 + core) * 16, 16), 16)
 
-    def landing(c):
-        return fb.at[c] if c < last else f_out
-
-    def finish(c):
-        for kind in (1, 2, 4, 5):
-            hop(c, kind).wait_recv()
-        for part, (r1, r2) in enumerate(((u2, dd), (d2, ud))):
-
-            def one(i, carry):
-                at = part * Q + i
-                total = hv[z, c * S + core * H + at].astype(F32) + pr[z, c * H + at].astype(F32)
-                total = total + (r1[c * Q + i].astype(F32) + r2[c * Q + i].astype(F32))
-                for k in range(jn // 128):
-                    at_row = pl.ds(pl.multiple_of(at * rows, rows), rows)
-                    xf[k, at_row, :] = total[:, k * 128 : (k + 1) * 128]
-                return carry
-
-            lax.fori_loop(0, Q, one, 0)
-        for level in range(8):
-            for k in range(jn // 128):
-                north = []
-                south = []
-                for p in range(2):
-                    even = xf[k, pl.ds(p * 16 + level, H, stride=rows), :]
-                    odd = xf[k, pl.ds(p * 16 + 8 + level, H, stride=rows), :]
-                    north.append(even + odd)
-                    south.append(even - odd)
-                at_row = slice(level * 16, (level + 1) * 16)
-                at = k * 128
-                xb[at_row, at : at + 128] = jnp.concatenate(north, axis=0).astype(BF16)
-                xb[at_row, jn + at : jn + at + 128] = jnp.concatenate(south, axis=0).astype(BF16)
-        lanes = gb.shape[4]
+    def fill(s, total):
+        even = jnp.concatenate([total[0:8], total[16:24]], axis=0)
+        odd = jnp.concatenate([total[8:16], total[24:32]], axis=0)
+        at = pl.ds(pl.multiple_of(s * 16, 16), 16)
+        xn[at, 0:jn] = (even + odd).astype(BF16)
+        xn[at, jn:] = (even - odd).astype(BF16)
+
+    def spread(box, land, recv_sem, send_sem):
+        for k in range(2 * jn // 256):
+            at = slice(k * 256, (k + 1) * 256)
+            xb[:, at] = jnp.dot(perm[...], xn[:, at], preferred_element_type=F32).astype(BF16)
+        lanes = box.shape[3]
 
         def pick(i, carry):
             pairs = ma_n // 2
@@ -285,7 +268,7 @@
                     ]
                     if lanes > ln * rb:
                         parts.append(jnp.zeros((16, lanes - ln * rb), F32))
-                    gb[c, tc, peer] = jnp.concatenate(parts, axis=1).astype(BF16)
+                    box[tc, peer] = jnp.concatenate(parts, axis=1).astype(BF16)
             for k in range(2):
                 peer = m2 * 2 + k
                 for tc in range(2):
@@ -293,24 +276,110 @@
                     @pl.when(jnp.logical_or(peer != me_ma, tc != core))
                     def _():
                         pltpu.make_async_remote_copy(
-                            src_ref=gb.at[c, tc, peer],
-                            dst_ref=landing(c).at[place, :],
-                            send_sem=a2a_s,
-                            recv_sem=a2a_r.at[c],
+                            src_ref=box.at[tc, peer],
+                            dst_ref=land.at[place, :],
+                            send_sem=send_sem,
+                            recv_sem=recv_sem,
                             device_id={"ma": peer, "lev": z * 2 + tc},
                             device_id_type=MESH,
                         ).start()
 
             return carry
 
-        lax.fori_loop(0, ma_n // 2, pick, 0)
-        if c < last:
-            landing(c)[place, :] = gb[c, core, me_ma]
-        else:
-            pltpu.make_async_copy(gb.at[c, core, me_ma], f_out.at[place, :], out_sem.at[2]).start()
+        lax.fori_loop(0, ma_n // 2, pick, 0, unroll=2 if ma_n > 2 else 1)
+        land[place, :] = box[core, me_ma]
+
+    def finish(c):
+        for kind in (1, 2, 4, 5):
+            hop(c, kind).wait_recv()
+        for part, (r1, r2) in enumerate(((u2, dd), (d2, ud))):
+
+            def one(i, carry):
+                at = part * Q + i
+                total = hv[z, c * S + core * H + at].astype(F32) + pr[z, c * H + at].astype(F32)
+                fill(at, total + (r1[c * Q + i].astype(F32) + r2[c * Q + i].astype(F32)))
+                return carry
+
+            lax.fori_loop(0, Q, one, 0)
+        spread(gb.at[c], fb.at[c], a2a_r.at[c], a2a_s)
+
+    hk = kc // 2
+
+    def early(k):
+        plane = (zo, zu, zd, z)[k]
+
+        def one(i, carry):
+            total = hv[plane, last * S + core * H + i].astype(F32)
+            fill(i, total + pr[plane, last * H + i].astype(F32))
+            return carry
+
+        lax.fori_loop(0, H, one, 0)
+        spread(gbs.at[k], sa.at[k], a2a_r.at[last + k], a2a_s2)
+
+    def arrived(k):
+        whole = sa.at[k, pl.ds(0, kc - 16)]
+        pltpu.make_async_copy(whole, whole, a2a_r.at[last + k]).wait()
+
+    def late_hop(kind):
+        k = (0, 1, 1, 0, 2, 2)[kind]
+        part = (0, 1, 0, 1, 0, 1)[kind]
+        return pltpu.make_async_remote_copy(
+            src_ref=sa.at[k, pl.ds(part * hk, hk)],
+            dst_ref=sbox.at[kind],
+            send_sem=ring_s.at[last, kind],
+            recv_sem=ring_r.at[last, kind],
+            device_id={"lev": up if kind < 3 else down},
+            device_id_type=MESH,
+        )
+
+    def add_rows(k, part, *kinds):
+        def one(i, carry):
+            at = pl.ds(pl.multiple_of(part * hk + i * 32, 32), 32)
+            other = pl.ds(pl.multiple_of(i * 32, 32), 32)
+            total = sa[k, at, :].astype(F32)
+            for kind in kinds:
+                total = total + sbox[kind, other, :].astype(F32)
+            sa[k, at, :] = total.astype(BF16)
+            return carry
+
+        lax.fori_loop(0, hk // 32, one, 0)
+
+    def late_far():
+        arrived(0)
+        late_hop(0).start()
+        late_hop(3).start()
+
+    def late_near():
+        arrived(1)
+        late_hop(1).start()
+        arrived(2)
+        late_hop(4).start()
+
+    def late_relay():
+        late_hop(0).wait_recv()
+        add_rows(1, 0, 0)
+        late_hop(2).start()
+        late_hop(3).wait_recv()
+        add_rows(2, 1, 3)
+        late_hop(5).start()
+
+    def send_rows():
+        return pltpu.make_async_copy(sa.at[3], f_out, out_sem.at[2])
+
+    def late_finish():
+        arrived(3)
+        for kind in (1, 2, 4, 5):
+            late_hop(kind).wait_recv()
+        add_rows(3, 0, 2, 4)
+        add_rows(3, 1, 5, 1)
+        send_rows().start()
 
     def selection():
         step = 128
+        to = lax.broadcasted_iota(jnp.int32, (128, 128), 0)
+        came = lax.broadcasted_iota(jnp.int32, (128, 128), 1)
+        to = (to % 8) * 16 + (to // 8 % 2) * 8 + to // 16
+        perm[...] = jnp.where(to == came, F32(1.0), F32(0.0)).astype(BF16)
         for m2 in range(ma_n // 2):
             latp[m2] = jnp.full((1, 2 * RP), -1, jnp.int32)
             for k in range(2):
@@ -349,7 +418,7 @@
             tb[at, half:] = jnp.concatenate([flip, flip], axis=0).astype(BF16)
             return carry
 
-        lax.fori_loop(0, per, one, 0, unroll=2)
+        lax.fori_loop(0, per, one, 0, unroll=8 if per % 8 == 0 else 4)
 
     def send_table():
         return pltpu.make_async_copy(tb.at[pl.ds(last * kc, kc)], t_out, out_sem.at[0])
@@ -377,56 +446,67 @@
     far(0)
     stage(3)
     far(1)
-    stage(4)
+    stage(8)
     relay(0)
     near(1)
-    for c in range(2, nc):
-        stage(2 * c + 1)
-        if c == 2:
-            for cp in small[3:]:
-                cp.wait()
-            mcol[...] = jnp.transpose(
-                jnp.broadcast_to(wave_v[...].reshape(1, mn).astype(F32), (8, mn))
-            )
-            selection()
-        if c >= 3:
-            finish(c - 3)
-            table(c - 3)
-        if c >= 4:
-            along(c - 4)
-        far(c)
-        if c < last:
-            stage(2 * c + 2)
-        relay(c - 1)
-        near(c)
-    table(last - 2)
-    table(last - 1)
-    table(last)
+    stage(4)
+    stage(5)
+    for cp in small[3:]:
+        cp.wait()
+    mcol[...] = jnp.transpose(jnp.broadcast_to(wave_v[...].reshape(1, mn).astype(F32), (8, mn)))
+    far(2)
+    stage(9)
+    stage(6)
+    relay(1)
+    near(2)
+    selection()
+    swap(8).wait_recv()
+    swap(9).wait_recv()
+    early(0)
+    stage(7)
+    early(1)
+    far(3)
+    early(2)
+    relay(2)
+    near(3)
+    finish(0)
+    early(3)
+    late_far()
+    finish(1)
+    relay(3)
+    late_near()
+    table(0)
+    finish(2)
+    table(1)
+    late_relay()
+    along(0)
+    finish(3)
+    table(4)
     send_table().start()
-    finish(last - 2)
-    along(last - 3)
-    relay(last)
-    finish(last - 1)
-    along(last - 2)
-    finish(last)
-    along(last - 1)
+    table(2)
+    table(3)
+    along(1)
+    along(2)
+    late_finish()
+    along(3)
     send_acc().start()
 
     for u in range(2 * nc):
         swap(u).wait_send()
-    for u in range(2 * nc - DEPTH, 2 * nc):
+    for u in ORDER[-DEPTH:]:
         for cp in keep(u):
             cp.wait()
-    for c in range(nc):
-        for kind in range(6):
+    for kind in range(6):
+        for c in range(last):
             hop(c, kind).wait_send()
+        late_hop(kind).wait_send()
     send_table().wait()
     send_acc().wait()
-    pltpu.make_async_copy(gb.at[last, core, me_ma], f_out.at[place, :], out_sem.at[2]).wait()
-    flat = gb.reshape(nc * 2 * ma_n, 16, gb.shape[4]).at[pl.ds(0, nc * (2 * ma_n - 1))]
-    pltpu.make_async_copy(flat, flat, a2a_s).wait()
-    whole = f_out.at[pl.ds(0, kc - 16)]
-    pltpu.make_async_copy(whole, whole, a2a_r.at[last]).wait()
+    send_rows().wait()
+    for box, sem in ((gb, a2a_s), (gbs, a2a_s2)):
+        n = box.shape[0]
+        flat = box.reshape(n * 2 * ma_n, 16, box.shape[4]).at[pl.ds(0, n * (2 * ma_n - 1))]
+        pltpu.make_async_copy(flat, flat, sem).wait()
 
 
 def grid_kernel(f_h, t_h, acc_h, kept_h, new_h, out_h, f, t, acc, kept, lhs, obuf, in_sem, keep_sem, out_sem):
@@ -503,7 +583,7 @@
     smem = pl.BlockSpec(memory_space=pltpu.SMEM)
     vmem = pl.BlockSpec(memory_space=pltpu.VMEM)
     hbm = pl.BlockSpec(memory_space=pl.ANY)
-    box = pltpu.VMEM((nc * Q, 32, jn), BF16)
+    box = pltpu.VMEM(((nc - 1) * Q, 32, jn), BF16)
     dma = pltpu.SemaphoreType.DMA
     f, t, acc, kept = pl.pallas_call(
         transform_kernel,
@@ -528,11 +608,15 @@
             pltpu.VMEM((zn, ns, 32, jn), BF16),
             pltpu.VMEM((zn, ns // 2, 32, jn), BF16),
             box, box, box, box, box, box,
-            pltpu.VMEM((jn // 128, H * 32, 128), F32),
+            pltpu.VMEM((128, 128), BF16),
+            pltpu.VMEM((128, 2 * jn), BF16),
             pltpu.VMEM((128, 2 * jn), BF16),
             pltpu.VMEM((ma_n // 2, 2 * jn, 2 * RP), BF16),
-            pltpu.VMEM((nc, 2, ma_n, 16, lanes), BF16),
+            pltpu.VMEM((nc - 1, 2, ma_n, 16, lanes), BF16),
+            pltpu.VMEM((4, 2, ma_n, 16, lanes), BF16),
             pltpu.VMEM((nc - 1, kc, lanes), BF16),
+            pltpu.VMEM((4, kc, lanes), BF16),
+            pltpu.VMEM((6, kc // 2, lanes), BF16),
             pltpu.VMEM((kn, half + RP), BF16),
             pltpu.VMEM((mn, 8), F32),
             pltpu.VMEM((ma_n // 2, 1, 2 * RP), jnp.int32),
@@ -547,7 +631,8 @@
             dma((nc, 6)),
             dma((nc, 6)),
             dma,
-            dma((nc,)),
+            dma,
+            dma((nc + 3,)),
             dma((3,)),
         ],
         compiler_params=pltpu.CompilerParams(

time: 83 us -> 81 us (0.976)
  Pallas kernels: 82.1 us -> 80.1 us
    pallas_call x1, Pallas kernels: 75.6 us -> 73.6 us  [body(): pl.pallas_call(transform_kernel, out_shape=(jax.ShapeDtypeStruct((kc, lan...]
where the time goes in v4:
time: 81 us; the launch traced here: 80.9 us
  Pallas kernels  80.1 us (99%)
    pallas_call x1, Pallas kernels, body(): pl.pallas_call(transform_kernel, out_shape=(jax.ShapeDtypeStruct((kc, lan...  73.6 us
    pallas_call x1, Pallas kernels, body(): pl.pallas_call(grid_kernel, out_shape=(jax.ShapeDtypeStruct((nc, S, 2, le...  6.48 us

profile of v4, /device:TPU:1, one launch (start us, length us, event | category | flops | bytes accessed | tf_op | source)
XLA Modules:
  0.0 80.9 jit_solution(15436941446085760357)
XLA Ops:
  0.6 73.6 %transform.1 = (bf16[512,384]{1,0:T(8,128)(2,1)}, bf16[512,1408]{1,0:T(8,128)(2,1)}, bf16[640,1280]{1,0:T(8,128)(2,1)}, f32[5,2,2,4,2,32,160]{6,5,4,3,2,1,0:T(8,128)}) custom-call(s32[1280]{0:T(1024)} %wave_h.1, s32[1280]{0:T(1024)} %lat_h.1, f32[32]{0:T(128)} %decay_h.1, f32[160]{0:T(256)} %amp_h.1, f32[5,2,2,4,2,32,160]{6,5,4,3,2,1,0:T(8,128)} %bitcast.7, ...), custom_call_target="tpu_custom_call" | custom-call | tf_op jit(solution)/shard_map/transform/pallas_call | solution.py:588
  74.2 6.5 %grid_rows.1 = (f32[5,16,2,32,160]{4,3,2,1,0:T(8,128)}, bf16[4,80,2560]{2,1,0:T(8,128)(2,1)}) custom-call(bf16[512,384]{1,0:T(8,128)(2,1)} %get-tuple-element.8.f_h, bf16[512,1408]{1,0:T(8,128)(2,1)} %get-tuple-element.9.t_h, bf16[640,1280]{1,0:T(8,128)(2,1)} %get-tuple-element.10.acc_h, f32[5,16,2,32,160]{4,3,2,1,0:T(8,128)} %bitcast.6), custom_call_target="tpu_custom_call" | custom-call | tf_op jit(solution)/shard_map/grid_rows/pallas_call | solution.py:650
